TPU v7x, 32 devices: a whole 2x2x4 slice. The times are simulated.
32 devices in a mesh: dp: 16 (over z, x, core), stream: 2 (over y).
Axes of the slice: x: 2, y: 2, z: 4, core: 2. Of those that a mesh axis runs over, the one named last changes fastest.
Arguments:
- tokens: bfloat16 [80, 2, 200, 768], P('dp', 'stream'), may hold values from -6 to 6
- text_segment: int32 [80, 200], P('dp'), may hold values from 0 to 5, as said below
- ln1_gain: float32 [768], replicated, may hold values from 0.5 to 1.5
- ln1_bias: float32 [768], replicated, may hold values from -3 to 3
- qkv_weight: bfloat16 [768, 2304], replicated, may hold values from -0.3125 to 0.3125
- out_weight: bfloat16 [768, 768], replicated, may hold values from -0.625 to 0.625
- attn_scale: float32 [768], replicated, may hold values from 0.25 to 1.75
- ffn_scale: float32 [768], replicated, may hold values from 0.25 to 1.75
- ln2_gain: float32 [2, 768], P('stream'), may hold values from 0.5 to 1.5
- ln2_bias: float32 [2, 768], P('stream'), may hold values from -3 to 3
- expert_in: bfloat16 [2, 768, 3072], P('stream'), may hold values from -0.21875 to 0.21875
- expert_out: bfloat16 [2, 3072, 768], P('stream'), may hold values from -0.15625 to 0.15625
- out_cot: bfloat16 [80, 2, 200, 768], P('dp', 'stream'), may hold values from -6 to 6
Outputs:
- block_out: bfloat16 [80, 2, 200, 768], P('dp', 'stream')
- tokens_grad: bfloat16 [80, 2, 200, 768], P('dp', 'stream')
- ln1_gain_grad: float32 [768], replicated
- ln1_bias_grad: float32 [768], replicated
- qkv_weight_grad: float32 [768, 2304], replicated
- out_weight_grad: float32 [768, 768], replicated
- attn_scale_grad: float32 [768], replicated
- ffn_scale_grad: float32 [768], replicated
- ln2_gain_grad: float32 [2, 768], P('stream')
- ln2_bias_grad: float32 [2, 768], P('stream')
- expert_in_grad: float32 [2, 768, 3072], P('stream')
- expert_out_grad: float32 [2, 3072, 768], P('stream')
Inputs may be any that keep to these rules, and one draw needn't show every extreme that they name: `text_segment`: in each group the text slots hold the captions numbered below 5 in order, each of 1 to 39 slots, followed by padding slots numbered 5.
All inputs are finite; a program needn't handle non-finite values.
Results may differ from a plain program's by a relative error of at most 0.015.
The roundings to bfloat16 on the way count: a program that leaves them out, or rounds other values in their place, can miss the bound.
Values may be sent and summed in bfloat16 or wider, within the bound.
A program may use at most 256 MiB of HBM per device.

v0:
```python
import jax
import jax.numpy as jnp
from jax import lax
from jax.sharding import PartitionSpec as P

HEADS = 12
HDIM = 64
PATCHES = 197
CAPTIONS = 5


EPSILON = 1e-05


def layer_norm(inputs, gain_row, bias_row):
    row_mean = jnp.mean(inputs, axis=-1, keepdims=True)
    centered = inputs - row_mean
    variance = jnp.mean(centered * centered, axis=-1, keepdims=True)
    return centered * lax.rsqrt(variance + EPSILON) * gain_row + bias_row


def gelu_exact(inputs):
    return jax.nn.gelu(inputs, approximate=False)


def contract_rows(left_side, right_side):
    return lax.dot_general(
        left_side, right_side, (((0,), (0,)), ((), ())), preferred_element_type=jnp.float32
    )


def times_transposed(left_side, right_side):
    return lax.dot_general(
        left_side, right_side, (((1,), (1,)), ((), ())), preferred_element_type=jnp.float32
    )


def shards(
    tokens,
    text_segment,
    ln1_gain,
    ln1_bias,
    qkv_weight,
    out_weight,
    attn_scale,
    ffn_scale,
    ln2_gain,
    ln2_bias,
    expert_in,
    expert_out,
    out_cot,
):
    group_count = tokens.shape[0]
    slot_count = tokens.shape[2]
    model_width = tokens.shape[3]
    row_count = group_count * slot_count
    score_scale = HDIM ** (-0.5)
    stream_index = lax.axis_index("stream")
    flat_rows = tokens.reshape(row_count, model_width).astype(jnp.float32)
    attn_in, ln1_pull = jax.vjp(layer_norm, flat_rows, ln1_gain, ln1_bias)
    attn_low = attn_in.astype(jnp.bfloat16)
    qkv = jnp.dot(attn_low, qkv_weight, preferred_element_type=jnp.float32).astype(jnp.bfloat16)
    qkv_heads = qkv.reshape(group_count, slot_count, 3, HEADS, HDIM)
    queries = qkv_heads[:, :, 0]
    pairs = qkv_heads[:, :, 1:].reshape(group_count, 1, slot_count, 2 * model_width)
    gathered = lax.all_gather(pairs, "stream", axis=1, tiled=True)
    both_heads = gathered.reshape(group_count, 2 * slot_count, 2, HEADS, HDIM)
    key_all = both_heads[:, :, 0]
    value_all = both_heads[:, :, 1]
    slot_index = lax.broadcasted_iota(jnp.int32, (slot_count,), 0)
    patch_key = slot_index < PATCHES
    text_key = text_segment < CAPTIONS
    same_caption = text_segment[:, :, None] == text_segment[:, None, :]
    patch_part = jnp.broadcast_to(patch_key[None, None, :], (group_count, slot_count, slot_count))
    image_text = jnp.broadcast_to(text_key[:, None, :], (group_count, slot_count, slot_count))
    text_part = jnp.where(stream_index == 0, image_text, same_caption)
    visible = jnp.concatenate([patch_part, text_part], axis=2)[:, None]

    def masked_scores():
        scores = (
            jnp.einsum("gqhe,gkhe->ghqk", queries, key_all, preferred_element_type=jnp.float32)
            * score_scale
        )
        return jnp.where(visible, scores, jnp.float32(-1e30))

    scores = masked_scores()
    row_max = jnp.max(scores, axis=-1, keepdims=True)
    exp_terms = jnp.exp(scores - row_max)
    row_total = jnp.sum(exp_terms, axis=-1, keepdims=True)
    weights = exp_terms / row_total
    log_total = row_max + jnp.log(row_total)
    mixed_heads = jnp.einsum(
        "ghqk,gkhe->gqhe",
        weights.astype(jnp.bfloat16),
        value_all,
        preferred_element_type=jnp.float32,
    )
    mixed_heads = mixed_heads.astype(jnp.bfloat16).reshape(row_count, model_width)
    attn_proj = jnp.dot(mixed_heads, out_weight, preferred_element_type=jnp.float32)
    residual = flat_rows + attn_scale * attn_proj
    in_matrix = expert_in[0]
    out_matrix = expert_out[0]
    ffn_in, ln2_pull = jax.vjp(layer_norm, residual, ln2_gain[0], ln2_bias[0])
    ffn_low = ffn_in.astype(jnp.bfloat16)
    pre_act = jnp.dot(ffn_low, in_matrix, preferred_element_type=jnp.float32)
    activation = gelu_exact(pre_act).astype(jnp.bfloat16)
    ffn_out = jnp.dot(activation, out_matrix, preferred_element_type=jnp.float32)
    block_out = (residual + ffn_scale * ffn_out).astype(jnp.bfloat16)
    grad_out = out_cot.reshape(row_count, model_width).astype(jnp.float32)
    ffn_scale_grad = jnp.sum(grad_out * ffn_out, axis=0)
    grad_ffn = (ffn_scale * grad_out).astype(jnp.bfloat16)
    expert_out_grad = contract_rows(activation, grad_ffn)
    grad_act = times_transposed(grad_ffn, out_matrix)
    _, gelu_pull = jax.vjp(gelu_exact, pre_act)
    grad_pre = gelu_pull(grad_act)[0].astype(jnp.bfloat16)
    expert_in_grad = contract_rows(ffn_low, grad_pre)
    grad_ffn_in = times_transposed(grad_pre, in_matrix)
    grad_resid_norm, ln2_gain_grad, ln2_bias_grad = ln2_pull(grad_ffn_in)
    grad_resid = grad_out + grad_resid_norm
    expert_total = lax.psum((expert_in_grad, expert_out_grad, ln2_gain_grad, ln2_bias_grad), "dp")
    attn_scale_grad = jnp.sum(grad_resid * attn_proj, axis=0)
    grad_proj = (attn_scale * grad_resid).astype(jnp.bfloat16)
    out_weight_grad = contract_rows(mixed_heads, grad_proj)
    grad_mix = times_transposed(grad_proj, out_weight).astype(jnp.bfloat16)
    grad_mix = grad_mix.reshape(group_count, slot_count, HEADS, HDIM)
    weights_again = jnp.exp(masked_scores() - log_total)
    grad_probs = jnp.einsum(
        "gqhe,gkhe->ghqk", grad_mix, value_all, preferred_element_type=jnp.float32
    )
    inner_sum = jnp.sum(weights_again * grad_probs, axis=-1, keepdims=True)
    grad_scores = (weights_again * (grad_probs - inner_sum)).astype(jnp.bfloat16)
    grad_query = (
        jnp.einsum("ghqk,gkhe->gqhe", grad_scores, key_all, preferred_element_type=jnp.float32)
        * score_scale
    )
    grad_query = grad_query.astype(jnp.bfloat16).reshape(row_count, model_width)
    grad_key = (
        jnp.einsum("ghqk,gqhe->gkhe", grad_scores, queries, preferred_element_type=jnp.float32)
        * score_scale
    )
    grad_value = jnp.einsum(
        "ghqk,gqhe->gkhe",
        weights_again.astype(jnp.bfloat16),
        grad_mix,
        preferred_element_type=jnp.float32,
    )
    key_terms = jnp.stack([grad_key, grad_value], axis=2).reshape(
        group_count, 2, slot_count, 2 * model_width
    )
    owned_grads = lax.psum_scatter(
        key_terms.astype(jnp.bfloat16), "stream", scatter_dimension=1, tiled=True
    ).astype(jnp.float32)
    owned_grads = owned_grads.reshape(row_count, 2 * model_width).astype(jnp.bfloat16)
    grad_qkv = jnp.concatenate([grad_query, owned_grads], axis=1)
    qkv_weight_grad = contract_rows(attn_low, grad_qkv)
    grad_attn_in = times_transposed(grad_qkv, qkv_weight)
    grad_rows_norm, ln1_gain_grad, ln1_bias_grad = ln1_pull(grad_attn_in)
    tokens_grad = (grad_resid + grad_rows_norm).astype(jnp.bfloat16).reshape(tokens.shape)
    small_grads = jnp.stack([ln1_gain_grad, ln1_bias_grad, attn_scale_grad, ffn_scale_grad], axis=0)
    shared_total = lax.psum((qkv_weight_grad, out_weight_grad, small_grads), ("dp", "stream"))
    small_total = shared_total[2]
    return (
        block_out.reshape(tokens.shape),
        tokens_grad,
        small_total[0],
        small_total[1],
        shared_total[0],
        shared_total[1],
        small_total[2],
        small_total[3],
        expert_total[2][None, :],
        expert_total[3][None, :],
        expert_total[0][None, :, :],
        expert_total[1][None, :, :],
    )


def solution(mesh):
    placed = (
        P("dp", "stream", None, None),
        P("dp", None),
        P(),
        P(),
        P(),
        P(),
        P(),
        P(),
        P("stream", None),
        P("stream", None),
        P("stream", None, None),
        P("stream", None, None),
        P("dp", "stream", None, None),
    )
    return jax.shard_map(
        shards,
        mesh=mesh,
        in_specs=placed,
        out_specs=(
            P("dp", "stream", None, None),
            P("dp", "stream", None, None),
            P(),
            P(),
            P(),
            P(),
            P(),
            P(),
            P("stream", None),
            P("stream", None),
            P("stream", None, None),
            P("stream", None, None),
        ),
        check_vma=False,
    )
```

profile of v0, /device:TPU:0, one launch (start us, length us, event | category | flops | bytes accessed | tf_op | source)
XLA Modules:
  0.0 1063.5 jit_solution(14414983165366514719)
XLA Ops:
  23.0 6.6 copy.61
  29.6 15.1 %reshape.175 = bf16[5,200,3,12,64]{1,0,4,3,2:T(8,128)(2,1)} reshape(bf16[1000,2304]{0,1:T(8,128)(2,1)} %copy.61) | data formatting | bytes 9216000 | tf_op jit(solution)/shard_map/reshape | solution.py:63
  50.8 7.2 copy.63
  66.8 72.7 %all-gather.2.cloned.1.call-done = bf16[5,2,200,1536]{3,2,0,1:T(8,128)(2,1)} async-done(((bf16[5,1,200,1536]{3,2,0,1:T(8,128)(2,1)}), bf16[5,2,200,1536]{3,2,0,1:T(8,128)(2,1)}) %all-gather.2.cloned.1.call-update) | async-done | bytes 6144016 | tf_op jit(solution)/shard_map/all_gather | solution.py:66
  139.5 20.2 %copy.64 = bf16[5,2,200,1536]{2,1,3,0:T(2,128)(2,1)} copy(bf16[5,2,200,1536]{3,2,0,1:T(8,128)(2,1)} %all-gather.2.cloned.1.call-done) | data formatting | bytes 12288000 | tf_op jit(solution)/shard_map/all_gather | solution.py:66
  159.7 13.1 %reshape.177 = bf16[5,400,2,12,64]{1,4,3,2,0:T(8,128)(2,1)} reshape(bf16[5,2,200,1536]{2,1,3,0:T(2,128)(2,1)} %copy.64) | data formatting | bytes 12288000 | tf_op jit(solution)/shard_map/reshape | solution.py:67
  172.8 15.1 %fusion.39 = (f32[5,12,200]{2,1,0:T(8,128)S(1)}, f32[5,12,200,400]{3,2,1,0:T(8,128)}) fusion(bf16[5,400,2,12,64]{1,4,3,2,0:T(8,128)(2,1)} %reshape.177, bf16[5,200,1,12,64]{1,0,4,3,2:T(8,128)(2,1)} %slice.34, pred[5,200,400]{2,1,0:T(8,128)(4,1)} %pad_add_fusion), kind=kOutput, calls=%fused_computation.101 | convolution fusion | flops 628787968 | bytes 26837888 | tf_op jit(solution)/shard_map/gqhe,gkhe->ghqk/dot_general | solution.py:81
  187.9 11.5 %fusion = f32[5,12,200]{2,1,0:T(8,128)S(1)} fusion(f32[5,12,200,400]{3,2,1,0:T(8,128)} %get-tuple-element.88, f32[5,12,200]{2,1,0:T(8,128)S(1)} %get-tuple-element.87), kind=kLoop, calls=%fused_computation.6 | loop fusion | flops 9588000 | bytes 19296000 | tf_op jit(solution)/shard_map/reduce_sum | solution.py:89
  199.5 11.2 %convert_bitcast_fusion.1 = bf16[5,200,12,64]{1,3,2,0:T(8,128)(2,1)S(1)} fusion(f32[5,12,200,400]{3,2,1,0:T(8,128)} %get-tuple-element.88, f32[5,12,200]{2,1,0:T(8,128)S(1)} %fusion, f32[5,12,200]{2,1,0:T(8,128)S(1)} %get-tuple-element.87, bf16[5,400,2,12,64]{1,4,3,2,0:T(8,128)(2,1)S(1)} %copy-done.3), kind=kOutput, calls=%fused_computation.76 | convolution fusion | flops 629568000 | bytes 24832000 | tf_op jit(solution)/shard_map/ghqk,gkhe->gqhe/dot_general | solution.py:92
  230.8 35.5 %multiply_convert_fusion.1 = (bf16[1000,3072]{1,0:T(8,128)(2,1)}, f32[1000,3072]{1,0:T(8,128)}, f32[1000,3072]{1,0:T(8,128)}) fusion(bf16[1,768,3072]{2,1,0:T(8,128)(2,1)} %param.23, f32[1000,768]{1,0:T(8,128)} %get-tuple-element.89, f32[768]{0:T(1024)S(1)} %reduce.5, f32[768]{0:T(1024)S(1)} %reduce.4, f32[1000]{0:T(1024)S(1)} %fusion.34, ...), kind=kOutput, calls=%fused_computation.13 | convolution fusion | flops 4922112000 | bytes 38524736 | tf_op jit(solution)/shard_map/dot_general | solution.py:105
  266.3 15.5 %add_convert_fusion = bf16[1000,3072]{1,0:T(8,128)(2,1)} fusion(f32[1000,3072]{1,0:T(8,128)} %get-tuple-element.81, f32[1000,3072]{1,0:T(8,128)} %get-tuple-element.91, bf16[1000,768]{1,0:T(8,128)(2,1)S(1)} %bitcast.116, bf16[1,3072,768]{2,1,0:T(8,128)(2,1)} %param.24), kind=kOutput, calls=%fused_computation.12 | convolution fusion | flops 4761600000 | bytes 36974592 | tf_op jit(solution)/shard_map/dot_general | solution.py:33
  281.8 10.3 multiply_reduce_fusion.1
  292.1 10.7 %fusion.26 = (f32[768]{0:T(1024)}, bf16[1000,768]{1,0:T(8,128)(2,1)}, f32[1000]{0:T(1024)S(1)}, f32[1000,768]{1,0:T(8,128)S(1)}, bf16[1000,768]{1,0:T(8,128)(2,1)}) fusion(bf16[5,1,200,768]{3,2,1,0:T(8,128)(2,1)S(1)} %copy-done.9, f32[1000,768]{1,0:T(8,128)S(1)} %copy-done.2, f32[768]{0:T(1024)S(1)} %copy-done.27, f32[1000]{0:T(1024)S(1)} %multiply_multiply_fusion.6, ...), kind=kOutput, calls=%fused_computation.56 | convolution fusion | flops 4730109952 | bytes 24711808 | tf_op jit(solution)/shard_map/dot_general | solution.py:107
  320.1 22.1 %multiply_reduce_fusion = (f32[5,12,200]{2,1,0:T(8,128)S(1)}, f32[5,12,200,400]{3,2,1,0:T(8,128)}) fusion(f32[5,12,200,400]{3,2,1,0:T(8,128)} %get-tuple-element.88, f32[5,12,200]{2,1,0:T(8,128)} %log_add_fusion, bf16[5,200,12,64]{1,3,2,0:T(8,128)(2,1)} %copy.70, bf16[5,400,2,12,64]{1,4,3,2,0:T(8,128)(2,1)} %reshape.177), kind=kOutput, calls=%fused_computation.1 | convolution fusion | flops 628787968 | bytes 49804160 | tf_op jit(solution)/shard_map/gqhe,gkhe->ghqk/dot_general | solution.py:127
  342.2 12.6 %convert_bitcast_fusion = bf16[5,400,1,12,64]{1,4,3,0,2:T(8,128)(2,1)} fusion(bf16[5,200,12,64]{1,3,2,0:T(8,128)(2,1)S(1)} %copy-done.6, f32[5,12,200,400]{3,2,1,0:T(8,128)} %get-tuple-element.88, f32[5,12,200]{2,1,0:T(8,128)S(1)} %copy-done.11), kind=kOutput, calls=%fused_computation.47 | convolution fusion | flops 625536000 | bytes 23856000 | tf_op jit(solution)/shard_map/ghqk,gqhe->gkhe/dot_general | solution.py:141
  354.8 16.3 %multiply_convert_fusion = bf16[5,12,200,400]{3,2,1,0:T(8,128)(2,1)S(1)} fusion(f32[5,12,200,400]{3,2,1,0:T(8,128)} %get-tuple-element.94, f32[5,12,200,400]{3,2,1,0:T(8,128)} %get-tuple-element.88, f32[5,12,200]{2,1,0:T(8,128)S(1)} %get-tuple-element.93, f32[5,12,200]{2,1,0:T(8,128)S(1)} %copy-done.11), kind=kLoop, calls=%fused_computation | loop fusion | flops 19200000 | bytes 48096000 | tf_op jit(solution)/shard_map/convert_element_type | solution.py:131
  379.4 7.4 pad_maximum_fusion
  386.9 7.5 copy.73
  394.3 13.2 %convert_element_type.107 = bf16[5,2,200,1536]{2,1,3,0:T(2,128)(2,1)} reshape(bf16[5,400,2,12,64]{1,4,3,2,0:T(8,128)(2,1)} %copy.73) | data formatting | bytes 12288000 | tf_op jit(solution)/shard_map/convert_element_type | solution.py:151
  407.5 19.6 %copy.74 = bf16[5,2,200,1536]{3,2,0,1:T(8,128)(2,1)} copy(bf16[5,2,200,1536]{2,1,3,0:T(2,128)(2,1)} %convert_element_type.107) | data formatting | bytes 12288000 | tf_op jit(solution)/shard_map/convert_element_type | solution.py:151
  427.2 11.2 %convolution_bitcast_fusion.1 = f32[1,768,3072]{2,1,0:T(8,128)} fusion(bf16[1000,3072]{1,0:T(8,128)(2,1)} %add_convert_fusion, f32[1000,768]{1,0:T(8,128)} %get-tuple-element.89, f32[768]{0:T(1024)S(1)} %reduce.5, f32[768]{0:T(1024)S(1)} %reduce.4, f32[1000]{0:T(1024)S(1)} %fusion.34, f32[1000]{0:T(1024)S(1)} %broadcast_multiply_fusion.1), kind=kOutput, calls=%fused_computation.31 | convolution fusion | flops 4722432000 | bytes 18667328 | tf_op jit(solution)/shard_map/dot_general | solution.py:27
  438.4 10.4 convolution_bitcast_fusion
  449.0 11.3 %fusion.32 = bf16[5,200,12,64]{1,3,2,0:T(8,128)(2,1)} fusion(bf16[5,12,200,400]{3,2,1,0:T(8,128)(2,1)} %copy-done.1, bf16[5,400,2,12,64]{1,4,3,2,0:T(8,128)(2,1)} %reshape.177), kind=kOutput, calls=%fused_computation.74 | convolution fusion | flops 615936000 | bytes 17756160 | tf_op jit(solution)/shard_map/ghqk,gkhe->gqhe/dot_general | solution.py:133
  477.9 25.0 %reduce-scatter.2.cloned.1.call-done = bf16[5,1,200,1536]{3,2,0,1:T(8,128)(2,1)} async-done(((bf16[5,2,200,1536]{3,2,0,1:T(8,128)(2,1)}), bf16[5,1,200,1536]{3,2,0,1:T(8,128)(2,1)}) %reduce-scatter.2.cloned.1.call-update) | async-done | bytes 3072016 | tf_op jit(solution)/shard_map/reduce_scatter | solution.py:150
  502.8 9.6 fusion.28
  516.9 36.8 %all-reduce.1 = (f32[1,768]{1,0:T(1,128)}, f32[1,768]{1,0:T(1,128)}) all-reduce(f32[1,768]{1,0:T(1,128)} %broadcast_in_dim.76, f32[1,768]{1,0:T(1,128)} %broadcast_in_dim.77), channel_id=1, replica_groups=mesh['dp'=16,'stream'=2] {'dp'}, use_global_device_ids=true, to_apply=%region_20.21 | all-reduce | flops 1536 | bytes 12288 | tf_op jit(solution)/shard_map/psum | solution.py:120
  553.7 7.9 multiply_reduce_fusion.3
  568.7 38.9 %psum.49 = f32[4,768]{1,0:T(4,128)S(1)} all-reduce(f32[4,768]{1,0:T(4,128)} %pad_maximum_fusion.4), channel_id=1, replica_groups=mesh['dp'=16,'stream'=2] {'dp','stream'}, use_global_device_ids=true, to_apply=%region_16.17 | all-reduce | flops 3072 | bytes 24576 | tf_op jit(solution)/shard_map/psum | solution.py:160
  612.6 225.5 %all-reduce.8.cloned.1.call-done = (f32[1,768,3072]{2,1,0:T(8,128)}, f32[1,3072,768]{2,1,0:T(8,128)}) async-done(((f32[1,768,3072]{2,1,0:T(8,128)}, f32[1,3072,768]{2,1,0:T(8,128)}), (f32[1,768,3072]{2,1,0:T(8,128)}, f32[1,3072,768]{2,1,0:T(8,128)})) %all-reduce.8.cloned.1.call-update) | async-done | bytes 18874384 | tf_op jit(solution)/shard_map/psum | solution.py:120
  838.1 197.6 %all-reduce.6.cloned.1.call-done = (f32[768,2304]{1,0:T(8,128)}, f32[768,768]{1,0:T(8,128)}) async-done(((f32[768,2304]{1,0:T(8,128)}, f32[768,768]{1,0:T(8,128)}), (f32[768,2304]{1,0:T(8,128)}, f32[768,768]{1,0:T(8,128)})) %all-reduce.6.cloned.1.call-update) | async-done | bytes 9437200 | tf_op jit(solution)/shard_map/psum | solution.py:160
  1035.7 6.6 copy.96
  1043.7 9.3 copy.98
  (129 shorter events, 116.0 us)
Async XLA Ops:
  7.2 10.5 copy-start
  7.2 132.3 %all-gather.2.cloned.1.call-start = ((), (), s32[]{:S(2)}) async-start(), calls=%async_computation.1 | async-start | bytes 9216000 | tf_op jit(solution)/shard_map/all_gather | solution.py:66
  11.7 11.3 %copy-start.16 = (f32[1000]{0:T(1024)}, f32[1000]{0:T(1024)S(1)}, u32[]{:S(2)}) copy-start(f32[1000]{0:T(1024)S(1)} %div.47) | copy-start | bytes 12004
  13.8 9.2 copy-start.20
  57.9 3.8 copy-start.28
  57.9 4.5 copy-start.15
  58.0 444.8 %reduce-scatter.2.cloned.1.call-start = ((), (), s32[]{:S(2)}) async-start(), calls=%async_computation.2 | async-start | bytes 9216000 | tf_op jit(solution)/shard_map/reduce_scatter | solution.py:150
  187.9 11.5 %copy-start.3 = (bf16[5,400,2,12,64]{1,4,3,2,0:T(8,128)(2,1)S(1)}, bf16[5,400,2,12,64]{1,4,3,2,0:T(8,128)(2,1)}, u32[]{:S(2)}) copy-start(bf16[5,400,2,12,64]{1,4,3,2,0:T(8,128)(2,1)} %reshape.177) | copy-start | bytes 18432004
  211.3 8.7 copy-start.22
  230.8 35.5 %copy-start.13 = (bf16[5,1,200,768]{3,2,1,0:T(8,128)(2,1)S(1)}, bf16[5,1,200,768]{3,2,1,0:T(8,128)(2,1)}, u32[]{:S(2)}) copy-start(bf16[5,1,200,768]{3,2,1,0:T(8,128)(2,1)} %fusion.25) | copy-start | bytes 4608004
  266.3 15.5 %copy-start.2 = (f32[1000,768]{1,0:T(8,128)S(1)}, f32[1000,768]{1,0:T(8,128)}, u32[]{:S(2)}) copy-start(f32[1000,768]{1,0:T(8,128)} %get-tuple-element.89) | copy-start | bytes 9216004
  281.8 10.3 copy-start.9
  281.8 10.3 copy-start.27
  281.8 10.3 copy-start.29
  292.1 10.7 %copy-start.5 = (f32[1000,768]{1,0:T(8,128)S(1)}, f32[1000,768]{1,0:T(8,128)}, u32[]{:S(2)}) copy-start(f32[1000,768]{1,0:T(8,128)} %get-tuple-element.90) | copy-start | bytes 9216004
  320.1 22.1 %copy-start.6 = (bf16[5,200,12,64]{1,3,2,0:T(8,128)(2,1)S(1)}, bf16[5,200,12,64]{1,3,2,0:T(8,128)(2,1)}, u32[]{:S(2)}) copy-start(bf16[5,200,12,64]{1,3,2,0:T(8,128)(2,1)} %copy.70) | copy-start | bytes 4608004
  320.1 22.1 %copy-start.11 = (f32[5,12,200]{2,1,0:T(8,128)S(1)}, f32[5,12,200]{2,1,0:T(8,128)}, u32[]{:S(2)}) copy-start(f32[5,12,200]{2,1,0:T(8,128)} %log_add_fusion) | copy-start | bytes 144004
  354.8 20.8 %copy-start.7 = (bf16[5,200,1,12,64]{1,0,4,3,2:T(8,128)(2,1)S(1)}, bf16[5,200,1,12,64]{1,0,4,3,2:T(8,128)(2,1)}, u32[]{:S(2)}) copy-start(bf16[5,200,1,12,64]{1,0,4,3,2:T(8,128)(2,1)} %slice.34) | copy-start | bytes 4608004
  371.1 4.5 copy-start.1
  427.1 411.0 %all-reduce.8.cloned.1.call-start = ((), (), s32[]{:S(2)}) async-start(), calls=%async_computation.4 | async-start | bytes 37748736 | tf_op jit(solution)/shard_map/psum | solution.py:120
  427.2 11.2 %copy-start.30 = (bf16[1000,768]{1,0:T(8,128)(2,1)S(1)}, bf16[1000,768]{1,0:T(8,128)(2,1)}, u32[]{:S(2)}) copy-start(bf16[1000,768]{1,0:T(8,128)(2,1)} %get-tuple-element.86) | copy-start | bytes 4608004
  448.8 586.9 %all-reduce.6.cloned.1.call-start = ((), (), s32[]{:S(2)}) async-start(), calls=%async_computation.3 | async-start | bytes 18874368 | tf_op jit(solution)/shard_map/psum | solution.py:160
  466.6 6.1 copy-start.24
  512.4 41.3 %copy-start.17 = (f32[1000]{0:T(1024)S(1)}, f32[1000]{0:T(1024)}, u32[]{:S(2)}) copy-start(f32[1000]{0:T(1024)} %copy-done.16) | copy-start | bytes 12004
  512.4 41.3 %copy-start.19 = (f32[1000]{0:T(1024)S(1)}, f32[1000]{0:T(1024)}, u32[]{:S(2)}) copy-start(f32[1000]{0:T(1024)} %copy-done.18) | copy-start | bytes 12004
  512.4 41.3 %copy-start.25 = (f32[768]{0:T(1024)S(1)}, f32[768]{0:T(1024)}, u32[]{:S(2)}) copy-start(f32[768]{0:T(1024)} %param.15) | copy-start | bytes 9220
  553.7 9.0 copy-start.21
  553.7 9.1 copy-start.4
  1035.7 6.6 copy-start.10
  1042.3 10.7 %slice-start = ((s8[9437184]{0:T(1024)(128)(4,1)}), s8[4194304]{0:T(1024)(128)(4,1)S(1)}, s32[]{:S(2)}) async-start(s8[9437184]{0:T(1024)(128)(4,1)} %bitcast.114), calls=%async_computation.5 | async-start | bytes 8388608
  1043.7 9.3 slice-start.1
  1043.7 9.3 slice-start.2
  (6 other events, 11.8 us)
Sparse Core Ops, SparseCore 0:
  58.1 81.4 all-gather.1
  427.2 75.5 reduce-scatter.1
  507.5 330.5 all-reduce.7
  844.5 191.1 all-reduce.5
where the time goes:
time: 1070 us; the launch traced here: 1060 us
  waiting for transfers between devices  521 us (49%)
  matrix products  207 us (19%)
  local copies, waits for them, and re-layouts  181 us (17%)
  blocking collectives  75.6 us (7%)
  other arithmetic  64.7 us (6%)
  between operations  14.3 us (1%)
    psum x1, waiting for transfers between devices, shards(): lax.psum((expert_in_grad, expert_out_grad, ln2_gain_grad, ln2_bias_grad),...  226 us
    psum x1, waiting for transfers between devices, shards(): lax.psum((qkv_weight_grad, out_weight_grad, small_grads), ('dp', 'stream'))  198 us
    all_gather x1, waiting for transfers between devices, shards(): gathered = lax.all_gather(pairs, 'stream', axis=1, tiled=True)  72.7 us
    psum x1, blocking collectives, shards(): lax.psum((qkv_weight_grad, out_weight_grad, small_grads), ('dp', 'stream'))  38.9 us
    psum x1, blocking collectives, shards(): lax.psum((expert_in_grad, expert_out_grad, ln2_gain_grad, ln2_bias_grad),...  36.8 us
    dot_general x4, matrix products, contract_rows(): lax.dot_general(left_side, right_side, (((0,), (0,)), ((), ())), preferre...  36.4 us
    dot_general x4, matrix products, times_transposed(): lax.dot_general(left_side, right_side, (((1,), (1,)), ((), ())), preferre...  36.2 us
    dot_general x1, matrix products, shards(): pre_act = jnp.dot(ffn_low, in_matrix, preferred_element_type=jnp.float32)  35.5 us
  transfers between devices with their start and end apart: 4, of which 4 were waited for; matrix products, arithmetic and copies ran while one was open for 9% of the time, Pallas kernels for 0%

commit v1 on v0

v1 whole, which is shorter than its diff:
```python
import functools

import jax
import jax.numpy as jnp
from jax import lax
from jax.experimental import pallas as pl
from jax.experimental.pallas import tpu as pltpu
from jax.sharding import PartitionSpec as P

HEADS = 12
HDIM = 64
PATCHES = 197
CAPTIONS = 5
EPSILON = 1e-05
LANES = 128
HIDDEN = -1e30
SCALE = HDIM ** (-0.5)
F32 = jnp.float32
BF16 = jnp.bfloat16


def layer_norm(inputs, gain_row, bias_row):
    row_mean = jnp.mean(inputs, axis=-1, keepdims=True)
    centered = inputs - row_mean
    variance = jnp.mean(centered * centered, axis=-1, keepdims=True)
    return centered * lax.rsqrt(variance + EPSILON) * gain_row + bias_row


def gelu_exact(inputs):
    return jax.nn.gelu(inputs, approximate=False)


def dot_nn(a, b):
    return lax.dot_general(a, b, (((1,), (0,)), ((), ())), preferred_element_type=F32)


def dot_nt(a, b):
    return lax.dot_general(a, b, (((1,), (1,)), ((), ())), preferred_element_type=F32)


def dot_tn(a, b):
    return lax.dot_general(a, b, (((0,), (0,)), ((), ())), preferred_element_type=F32)


def fill_bias(stream_ref, seg_row_ref, seg_col_ref, bias):
    slots = bias.shape[1]
    is_image = stream_ref[0] == 0
    seg_row = seg_row_ref[0]
    seg_col = seg_col_ref[0]
    key_slot = lax.broadcasted_iota(jnp.int32, (slots, slots), 0)
    patch = jnp.where(key_slot < PATCHES, 0.0, HIDDEN).astype(F32)
    text_col = jnp.where(seg_col < CAPTIONS, 0.0, HIDDEN).astype(F32)
    text = jnp.broadcast_to(text_col, (slots, slots))
    same = jnp.where(seg_col == seg_row, 0.0, HIDDEN).astype(F32)
    bias[0] = jnp.where(is_image, patch, same)
    bias[1] = jnp.where(is_image, text, patch)


def head_mask(shape, which):
    lane = lax.broadcasted_iota(jnp.int32, shape, 1)
    return (lane >= which * HDIM) & (lane < (which + 1) * HDIM)


def attend_kernel(stream_ref, seg_row_ref, seg_col_ref, qkv_ref, other_ref, mix_ref, lse_ref, bias):
    width = mix_ref.shape[2]
    fill_bias(stream_ref, seg_row_ref, seg_col_ref, bias)

    def pair_step(pair, carry):
        def cols(ref, part):
            return ref[0, :, pl.ds(pl.multiple_of(part * width + pair * LANES, LANES), LANES)]

        queries = cols(qkv_ref, 0) * jnp.asarray(SCALE, BF16)
        keys, values = cols(qkv_ref, 1), cols(qkv_ref, 2)
        keys_other, values_other = cols(other_ref, 0), cols(other_ref, 1)
        values_t, values_other_t = values.T, values_other.T
        mixed = []
        for which in range(2):
            q_head = jnp.where(head_mask(queries.shape, which), queries, jnp.zeros_like(queries))
            own = dot_nt(keys, q_head) + bias[0]
            other = dot_nt(keys_other, q_head) + bias[1]
            top = jnp.maximum(
                jnp.max(own, axis=0, keepdims=True), jnp.max(other, axis=0, keepdims=True)
            )
            own = jnp.exp(own - top)
            other = jnp.exp(other - top)
            total = jnp.sum(own, axis=0, keepdims=True) + jnp.sum(other, axis=0, keepdims=True)
            inverse = 1.0 / total
            lse_ref[0, pl.ds(pair * 2 + which, 1), :] = top + jnp.log(total)
            rows = slice(which * HDIM, (which + 1) * HDIM)
            mixed.append(
                dot_nn(values_t[rows], (own * inverse).astype(BF16))
                + dot_nn(values_other_t[rows], (other * inverse).astype(BF16))
            )
        mixed = jnp.concatenate(mixed, axis=0)
        mix_ref[0, :, pl.ds(pl.multiple_of(pair * LANES, LANES), LANES)] = mixed.T.astype(BF16)
        return carry

    lax.fori_loop(0, width // LANES, pair_step, 0)


def attend_back_kernel(
    stream_ref, seg_row_ref, seg_col_ref, qkv_ref, other_ref, gmix_ref, lse_ref, gq_ref, gkv_ref, bias
):
    width = gq_ref.shape[2]
    fill_bias(stream_ref, seg_row_ref, seg_col_ref, bias)

    def pair_step(pair, carry):
        def at(part):
            return pl.ds(pl.multiple_of(part * width + pair * LANES, LANES), LANES)

        queries = qkv_ref[0, :, at(0)] * jnp.asarray(SCALE, BF16)
        keys, values = qkv_ref[0, :, at(1)], qkv_ref[0, :, at(2)]
        keys_other, values_other = other_ref[0, :, at(0)], other_ref[0, :, at(1)]
        g_mix = gmix_ref[0, :, at(0)]
        keys_t, keys_other_t = keys.T, keys_other.T
        gq_t = []
        sums = [None] * 4
        for which in range(2):
            mask = head_mask(queries.shape, which)
            q_head = jnp.where(mask, queries, jnp.zeros_like(queries))
            g_head = jnp.where(mask, g_mix, jnp.zeros_like(g_mix))
            lse = lse_ref[0, pl.ds(pair * 2 + which, 1), :]
            p_own = jnp.exp(dot_nt(keys, q_head) + bias[0] - lse)
            p_other = jnp.exp(dot_nt(keys_other, q_head) + bias[1] - lse)
            gp_own = dot_nt(values, g_head)
            gp_other = dot_nt(values_other, g_head)
            inner = jnp.sum(p_own * gp_own, axis=0, keepdims=True) + jnp.sum(
                p_other * gp_other, axis=0, keepdims=True
            )
            ds_own = (p_own * (gp_own - inner)).astype(BF16)
            ds_other = (p_other * (gp_other - inner)).astype(BF16)
            rows = slice(which * HDIM, (which + 1) * HDIM)
            gq_t.append(dot_nn(keys_t[rows], ds_own) + dot_nn(keys_other_t[rows], ds_other))
            terms = [
                dot_nn(ds_own, q_head),
                dot_nn(p_own.astype(BF16), g_head),
                dot_nn(ds_other, q_head),
                dot_nn(p_other.astype(BF16), g_head),
            ]
            sums = [t if s is None else s + t for s, t in zip(sums, terms)]
        gq = jnp.concatenate(gq_t, axis=0).T * SCALE
        gq_ref[0, :, at(0)] = gq.astype(BF16)
        gkv_ref[0, 0, :, at(0)] = sums[0].astype(BF16)
        gkv_ref[0, 0, :, at(1)] = sums[1].astype(BF16)
        gkv_ref[1, 0, :, at(0)] = sums[2].astype(BF16)
        gkv_ref[1, 0, :, at(1)] = sums[3].astype(BF16)
        return carry

    lax.fori_loop(0, width // LANES, pair_step, 0)


def attention_specs(slots, width):
    return [
        pl.BlockSpec(memory_space=pltpu.SMEM),
        pl.BlockSpec((1, 1, slots), lambda g: (g, 0, 0)),
        pl.BlockSpec((1, slots, 1), lambda g: (g, 0, 0)),
        pl.BlockSpec((1, slots, 3 * width), lambda g: (g, 0, 0)),
        pl.BlockSpec((1, slots, 2 * width), lambda g: (g, 0, 0)),
    ]


def attend(stream, seg_row, seg_col, qkv, other):
    groups, slots, wide = qkv.shape
    width = wide // 3
    return pl.pallas_call(
        attend_kernel,
        grid=(groups,),
        in_specs=attention_specs(slots, width),
        out_specs=[
            pl.BlockSpec((1, slots, width), lambda g: (g, 0, 0)),
            pl.BlockSpec((1, 16, slots), lambda g: (g, 0, 0)),
        ],
        out_shape=[
            jax.ShapeDtypeStruct((groups, slots, width), BF16),
            jax.ShapeDtypeStruct((groups, 16, slots), F32),
        ],
        scratch_shapes=[pltpu.VMEM((2, slots, slots), F32)],
        compiler_params=pltpu.CompilerParams(vmem_limit_bytes=32 << 20),
        cost_estimate=pl.CostEstimate(
            flops=groups * 8 * slots * slots * width,
            bytes_accessed=groups * slots * width * 12,
            transcendentals=groups * HEADS * 2 * slots * slots,
        ),
        name="attend",
    )(stream, seg_row, seg_col, qkv, other)


def attend_back(stream, seg_row, seg_col, qkv, other, g_mix, lse):
    groups, slots, wide = qkv.shape
    width = wide // 3
    return pl.pallas_call(
        attend_back_kernel,
        grid=(groups,),
        in_specs=attention_specs(slots, width)
        + [
            pl.BlockSpec((1, slots, width), lambda g: (g, 0, 0)),
            pl.BlockSpec((1, 16, slots), lambda g: (g, 0, 0)),
        ],
        out_specs=[
            pl.BlockSpec((1, slots, width), lambda g: (g, 0, 0)),
            pl.BlockSpec((2, 1, slots, 2 * width), lambda g: (0, g, 0, 0)),
        ],
        out_shape=[
            jax.ShapeDtypeStruct((groups, slots, width), BF16),
            jax.ShapeDtypeStruct((2, groups, slots, 2 * width), BF16),
        ],
        scratch_shapes=[pltpu.VMEM((2, slots, slots), F32)],
        compiler_params=pltpu.CompilerParams(vmem_limit_bytes=32 << 20),
        cost_estimate=pl.CostEstimate(
            flops=groups * 20 * slots * slots * width,
            bytes_accessed=groups * slots * width * 24,
            transcendentals=groups * HEADS * 2 * slots * slots,
        ),
        name="attend_back",
    )(stream, seg_row, seg_col, qkv, other, g_mix, lse)


def shards(
    tokens,
    text_segment,
    ln1_gain,
    ln1_bias,
    qkv_weight,
    out_weight,
    attn_scale,
    ffn_scale,
    ln2_gain,
    ln2_bias,
    expert_in,
    expert_out,
    out_cot,
):
    groups, _, slots, width = tokens.shape
    rows = groups * slots
    swap = [(0, 1), (1, 0)]
    stream = lax.axis_index("stream").astype(jnp.int32).reshape(1)
    seg_row = text_segment.reshape(groups, 1, slots)
    seg_col = text_segment.reshape(groups, slots, 1)
    own_tokens = tokens.reshape(rows, width)
    other_tokens = lax.ppermute(own_tokens, "stream", swap)
    flat_rows = own_tokens.astype(F32)
    attn_in, ln1_pull = jax.vjp(layer_norm, flat_rows, ln1_gain, ln1_bias)
    attn_low = attn_in.astype(BF16)
    qkv = dot_nn(attn_low, qkv_weight).astype(BF16)
    other_low = layer_norm(other_tokens.astype(F32), ln1_gain, ln1_bias).astype(BF16)
    kv_weight = qkv_weight[:, width:]
    other_kv = dot_nn(other_low, kv_weight).astype(BF16)
    qkv = qkv.reshape(groups, slots, 3 * width)
    other_kv = other_kv.reshape(groups, slots, 2 * width)
    mixed, lse = attend(stream, seg_row, seg_col, qkv, other_kv)
    mixed = mixed.reshape(rows, width)
    attn_proj = dot_nn(mixed, out_weight)
    residual = flat_rows + attn_scale * attn_proj
    in_matrix = expert_in[0]
    out_matrix = expert_out[0]
    ffn_in, ln2_pull = jax.vjp(layer_norm, residual, ln2_gain[0], ln2_bias[0])
    ffn_low = ffn_in.astype(BF16)
    pre_act = dot_nn(ffn_low, in_matrix)
    activation = gelu_exact(pre_act).astype(BF16)
    ffn_out = dot_nn(activation, out_matrix)
    block_out = (residual + ffn_scale * ffn_out).astype(BF16)
    grad_out = out_cot.reshape(rows, width).astype(F32)
    ffn_scale_grad = jnp.sum(grad_out * ffn_out, axis=0)
    grad_ffn = (ffn_scale * grad_out).astype(BF16)
    expert_out_grad = dot_tn(activation, grad_ffn)
    grad_act = dot_nt(grad_ffn, out_matrix)
    _, gelu_pull = jax.vjp(gelu_exact, pre_act)
    grad_pre = gelu_pull(grad_act)[0].astype(BF16)
    expert_in_grad = dot_tn(ffn_low, grad_pre)
    grad_ffn_in = dot_nt(grad_pre, in_matrix)
    grad_resid_norm, ln2_gain_grad, ln2_bias_grad = ln2_pull(grad_ffn_in)
    grad_resid = grad_out + grad_resid_norm
    small_expert = jnp.stack([ln2_gain_grad, ln2_bias_grad], axis=0)
    expert_total = lax.psum(
        (expert_in_grad.astype(BF16), expert_out_grad.astype(BF16), small_expert.astype(BF16)), "dp"
    )
    attn_scale_grad = jnp.sum(grad_resid * attn_proj, axis=0)
    grad_proj = (attn_scale * grad_resid).astype(BF16)
    out_weight_grad = dot_tn(mixed, grad_proj)
    grad_mix = dot_nt(grad_proj, out_weight).astype(BF16).reshape(groups, slots, width)
    grad_query, grad_kv = attend_back(stream, seg_row, seg_col, qkv, other_kv, grad_mix, lse)
    grad_query = grad_query.reshape(rows, width)
    grad_kv = grad_kv.reshape(2, rows, 2 * width)
    back = dot_nt(grad_kv[1], kv_weight).astype(BF16)
    returned = lax.ppermute(back, "stream", swap)
    query_weight_grad = dot_tn(attn_low, grad_query)
    both_low = jnp.stack([attn_low, other_low], axis=0).reshape(2 * rows, width)
    kv_weight_grad = dot_tn(both_low, grad_kv.reshape(2 * rows, 2 * width))
    own_back = dot_nt(grad_query, qkv_weight[:, :width]) + dot_nt(grad_kv[0], kv_weight)
    grad_attn_in = own_back + returned.astype(F32)
    grad_rows_norm, ln1_gain_grad, ln1_bias_grad = ln1_pull(grad_attn_in)
    tokens_grad = (grad_resid + grad_rows_norm).astype(BF16).reshape(tokens.shape)
    small_grads = jnp.stack([ln1_gain_grad, ln1_bias_grad, attn_scale_grad, ffn_scale_grad], axis=0)
    shared_total = lax.psum(
        (
            query_weight_grad.astype(BF16),
            kv_weight_grad.astype(BF16),
            out_weight_grad.astype(BF16),
            small_grads.astype(BF16),
        ),
        ("dp", "stream"),
    )
    small_total = shared_total[3].astype(F32)
    small_expert = expert_total[2].astype(F32)
    qkv_weight_grad = jnp.concatenate([shared_total[0], shared_total[1]], axis=1).astype(F32)
    return (
        block_out.reshape(tokens.shape),
        tokens_grad,
        small_total[0],
        small_total[1],
        qkv_weight_grad,
        shared_total[2].astype(F32),
        small_total[2],
        small_total[3],
        small_expert[0][None, :],
        small_expert[1][None, :],
        expert_total[0].astype(F32)[None],
        expert_total[1].astype(F32)[None],
    )


def solution(mesh):
    rows4 = P("dp", "stream", None, None)
    ins = (
        rows4,
        P("dp", None),
        P(),
        P(),
        P(),
        P(),
        P(),
        P(),
        P("stream", None),
        P("stream", None),
        P("stream", None, None),
        P("stream", None, None),
        rows4,
    )
    outs = (
        rows4,
        rows4,
        P(),
        P(),
        P(),
        P(),
        P(),
        P(),
        P("stream", None),
        P("stream", None),
        P("stream", None, None),
        P("stream", None, None),
    )
    return jax.shard_map(shards, mesh=mesh, in_specs=ins, out_specs=outs, check_vma=False)
```

time: 1070 us -> 610 us (0.57)
  waiting for transfers between devices: 521 us -> 276 us
  local copies, waits for them, and re-layouts: 181 us -> 6.15 us
  matrix products: 207 us -> 128 us
  Pallas kernels: 0 us -> 57.1 us
  other arithmetic: 64.7 us -> 46.8 us
    psum x2, waiting for transfers between devices: 423 us -> 232 us  [the longest x1 182 us: shards(): lax.psum((expert_in_grad.astype(BF16), expert_out_grad.astype(BF16), smal...]
    dot_general x18 -> x16, matrix products: 207 us -> 128 us  [the longest x5 59.5 us: dot_nn(): lax.dot_general(a, b, (((1,), (0,)), ((), ())), preferred_element_type=F32)]
    all_gather x1 -> x0, waiting for transfers between devices: 72.7 us -> none  [shards(): gathered = lax.all_gather(pairs, 'stream', axis=1, tiled=True)]
    reshape x8 -> x2, local copies, waits for them, and re-layouts: 65.1 us -> 0.23 us  [the longest x1 0.22 us: shards(): seg_col = text_segment.reshape(groups, slots, 1)]
    pallas_call x0 -> x2, Pallas kernels: none -> 57.1 us  [the longest x1 34.2 us: attend_back(): pl.pallas_call(attend_back_kernel, grid=(groups,), in_specs=attention_spe...]
    ppermute x0 -> x2, waiting for transfers between devices: none -> 44.5 us  [the longest x1 24.6 us: shards(): returned = lax.ppermute(back, 'stream', swap)]
    convert_element_type x4 -> x0, local copies, waits for them, and re-layouts: 42.5 us -> none  [the longest x2 32.7 us: shards(): key_terms.astype(jnp.bfloat16)]
    reduce_scatter x1 -> x0, waiting for transfers between devices: 25 us -> none  [shards(): lax.psum_scatter(key_terms.astype(jnp.bfloat16), 'stream', scatter_dimens...]
where the time goes in v1:
time: 610 us; the launch traced here: 603 us
  waiting for transfers between devices  276 us (45%)
  matrix products  128 us (21%)
  blocking collectives  69 us (11%)
  Pallas kernels  57.1 us (9%)
  other arithmetic  46.8 us (8%)
  between operations  15.2 us (2%)
  local copies, waits for them, and re-layouts  6.15 us (1%)
    psum x1, waiting for transfers between devices, shards(): lax.psum((expert_in_grad.astype(BF16), expert_out_grad.astype(BF16), smal...  182 us
    dot_general x5, matrix products, dot_nn(): lax.dot_general(a, b, (((1,), (0,)), ((), ())), preferred_element_type=F32)  59.5 us
    psum x1, waiting for transfers between devices, shards(): lax.psum((query_weight_grad.astype(BF16), kv_weight_grad.astype(BF16), ou...  49.9 us
    psum x1, blocking collectives, shards(): lax.psum((query_weight_grad.astype(BF16), kv_weight_grad.astype(BF16), ou...  37.1 us
    dot_general x6, matrix products, dot_nt(): lax.dot_general(a, b, (((1,), (1,)), ((), ())), preferred_element_type=F32)  35.8 us
    pallas_call x1, Pallas kernels, attend_back(): pl.pallas_call(attend_back_kernel, grid=(groups,), in_specs=attention_spe...  34.2 us
    dot_general x5, matrix products, dot_tn(): lax.dot_general(a, b, (((0,), (0,)), ((), ())), preferred_element_type=F32)  32.3 us
    psum x1, blocking collectives, shards(): lax.psum((expert_in_grad.astype(BF16), expert_out_grad.astype(BF16), smal...  31.9 us
  transfers between devices with their start and end apart: 4, of which 4 were waited for; matrix products, arithmetic and copies ran while one was open for 9% of the time, Pallas kernels for 0%

profile of v1, /device:TPU:0, one launch (start us, length us, event | category | flops | bytes accessed | tf_op | source)
XLA Modules:
  0.0 603.0 jit_solution(9253074006394207080)
XLA Ops:
  7.3 3.1 collective-permute-start
  15.2 3.0 fusion.33
  19.9 4.5 convolution_convert_fusion
  24.5 19.8 %collective-permute-done = bf16[1000,768]{1,0:T(8,128)(2,1)} collective-permute-done((bf16[1000,768]{1,0:T(8,128)(2,1)}, bf16[1000,768]{1,0:T(8,128)(2,1)}, u32[]{:S(2)}, u32[]{:S(2)}) %collective-permute-start) | collective-permute-done | bytes 1536032 | tf_op jit(solution)/shard_map/ppermute | solution.py:240
  48.0 4.3 convolution_convert_fusion.3
  52.4 23.0 %attend.1 = (bf16[5,200,768]{2,1,0:T(8,128)(2,1)S(1)}, f32[5,16,200]{2,1,0:T(8,128)S(1)}) custom-call(s32[1]{0:T(128)} %bitcast.1.stream_ref, s32[5,1,200]{2,1,0:T(1,128)S(1)} %reshape.312.seg_row_ref, s32[5,200,1]{2,1,0:T(8,128)S(1)} %copy.27.seg_col_ref, bf16[5,200,2304]{2,1,0:T(8,128)(2,1)S(1)} %bitcast.79, bf16[5,200,1536]{2,1,0:T(8,128)(2,1)S(1)} %bitcast.83), custom_call_target="tpu_custom_call" | custom-call | flops 1228800000 | bytes 9216000 | tf_op jit(solution)/shard_map/attend/pallas_call | solution.py:165
  75.4 4.1 convert_add_fusion
  81.6 2.5 multiply_reduce_fusion.3
  84.4 35.6 %multiply_convert_fusion = (bf16[1000,3072]{1,0:T(8,128)(2,1)}, f32[1000,3072]{1,0:T(8,128)}, f32[1000,3072]{1,0:T(8,128)}) fusion(bf16[1,768,3072]{2,1,0:T(8,128)(2,1)} %param.23, f32[1000,768]{1,0:T(8,128)S(1)} %copy-done.8, f32[768]{0:T(1024)S(1)} %reduce.5, f32[768]{0:T(1024)S(1)} %reduce.4, f32[1000]{0:T(1024)S(1)} %fusion.50, ...), kind=kOutput, calls=%fused_computation.3 | convolution fusion | flops 4922112000 | bytes 38524736 | tf_op jit(solution)/shard_map/dot_general | solution.py:34
  120.0 15.5 %add_convert_fusion = bf16[1000,3072]{1,0:T(8,128)(2,1)} fusion(f32[1000,3072]{1,0:T(8,128)} %get-tuple-element.64, f32[1000,3072]{1,0:T(8,128)} %get-tuple-element.80, bf16[1000,768]{1,0:T(8,128)(2,1)S(1)} %bitcast.96, bf16[1,3072,768]{2,1,0:T(8,128)(2,1)} %param.24), kind=kOutput, calls=%fused_computation.2 | convolution fusion | flops 4761600000 | bytes 36974592 | tf_op jit(solution)/shard_map/dot_general | solution.py:38
  135.6 11.2 %multiply_reduce_fusion = (bf16[768]{0:T(1024)(128)(2,1)S(1)}, f32[1000]{0:T(1024)S(1)}, bf16[768]{0:T(1024)(128)(2,1)S(1)}, f32[1000,768]{1,0:T(8,128)}) fusion(f32[1000,768]{1,0:T(8,128)S(1)} %copy-done.8, f32[1000]{0:T(1024)S(1)} %fusion.50, f32[1000]{0:T(1024)S(1)} %broadcast_multiply_fusion.1, f32[768]{0:T(1024)S(1)} %reduce.4, ...), kind=kOutput, calls=%fused_computation.62 | convolution fusion | flops 4724732928 | bytes 17024736 | tf_op jit(solution)/shard_map/dot_general | solution.py:38
  146.8 10.9 %fusion.34 = (bf16[768]{0:T(1024)(128)(2,1)S(1)}, bf16[1000,768]{1,0:T(8,128)(2,1)}, f32[1000]{0:T(1024)S(1)}, f32[1000,768]{1,0:T(8,128)S(1)}, bf16[1000,768]{1,0:T(8,128)(2,1)}) fusion(bf16[5,1,200,768]{3,2,1,0:T(8,128)(2,1)S(1)} %copy-done.11, f32[1000,768]{1,0:T(8,128)S(1)} %copy-done.8, f32[768]{0:T(1024)S(1)} %copy-done.33, ...), kind=kOutput, calls=%fused_computation.60 | convolution fusion | flops 4730109952 | bytes 24710272 | tf_op jit(solution)/shard_map/dot_general | solution.py:34
  161.4 34.2 %attend_back.1 = (bf16[5,200,768]{2,1,0:T(8,128)(2,1)S(1)}, bf16[2,5,200,1536]{3,2,1,0:T(8,128)(2,1)S(1)}) custom-call(s32[1]{0:T(128)} %bitcast.1.stream_ref, s32[5,1,200]{2,1,0:T(1,128)S(1)} %reshape.312.seg_row_ref, s32[5,200,1]{2,1,0:T(8,128)S(1)} %copy.27.seg_col_ref, bf16[5,200,2304]{2,1,0:T(8,128)(2,1)S(1)} %bitcast.82, ...), custom_call_target="tpu_custom_call" | custom-call | flops 3072000000 | bytes 18432000 | tf_op jit(solution)/shard_map/attend_back/pallas_call | solution.py:191
  197.6 2.6 fusion.41
  202.7 2.5 convolution_convert_fusion.7
  205.2 2.6 convolution_convert_fusion.6
  207.8 2.6 fusion.38
  210.4 24.6 %collective-permute-done.1 = bf16[1000,768]{1,0:T(8,128)(2,1)S(1)} collective-permute-done((bf16[1000,768]{1,0:T(8,128)(2,1)S(1)}, bf16[1000,768]{1,0:T(8,128)(2,1)S(1)}, u32[]{:S(2)}, u32[]{:S(2)}) %collective-permute-start.1) | collective-permute-done | bytes 1536032 | tf_op jit(solution)/shard_map/ppermute | solution.py:285
  235.1 2.4 fusion.27
  237.5 3.8 fusion.52
  241.6 6.7 %convolution_convert_fusion.4 = bf16[768,1536]{1,0:T(8,128)(2,1)} fusion(bf16[2000,768]{1,0:T(8,128)(2,1)S(1)} %bitcast.94, bf16[2000,1536]{1,0:T(8,128)(2,1)S(1)} %bitcast.76), kind=kOutput, calls=%fused_computation.45 | convolution fusion | flops 4719771648 | bytes 11575296 | tf_op jit(solution)/shard_map/dot_general | solution.py:42
  248.3 10.4 %fusion.14 = bf16[1,768,3072]{2,1,0:T(8,128)(2,1)} fusion(bf16[1000,3072]{1,0:T(8,128)(2,1)} %add_convert_fusion, f32[1000,768]{1,0:T(8,128)} %get-tuple-element.78, f32[768]{0:T(1024)S(1)} %reduce.5, f32[768]{0:T(1024)S(1)} %reduce.4, f32[1000]{0:T(1024)S(1)} %fusion.50, f32[1000]{0:T(1024)S(1)} %broadcast_multiply_fusion.1), kind=kOutput, calls=%fused_computation.30 | convolution fusion | flops 4724791296 | bytes 13948736 | tf_op jit(solution)/shard_map/dot_general | solution.py:42
  258.7 10.2 %fusion.15 = bf16[1,3072,768]{2,1,0:T(8,128)(2,1)} fusion(bf16[1000,3072]{1,0:T(8,128)(2,1)} %get-tuple-element.63, bf16[1000,768]{1,0:T(8,128)(2,1)S(1)} %copy-done.39), kind=kOutput, calls=%fused_computation.31 | convolution fusion | flops 4720951296 | bytes 12398592 | tf_op jit(solution)/shard_map/dot_general | solution.py:42
  269.0 31.9 %psum.53 = bf16[2,768]{1,0:T(2,128)(2,1)S(1)} all-reduce(bf16[2,768]{1,0:T(2,128)(2,1)S(1)} %pad_maximum_fusion.2), channel_id=1, replica_groups=mesh['dp'=16,'stream'=2] {'dp'}, use_global_device_ids=true, to_apply=%region_20.0 | all-reduce | flops 1536 | bytes 6144 | tf_op jit(solution)/shard_map/psum | solution.py:274
  301.6 37.1 %psum.49 = bf16[4,768]{1,0:T(4,128)(2,1)S(1)} all-reduce(bf16[4,768]{1,0:T(4,128)(2,1)S(1)} %pad_maximum_fusion.1), channel_id=1, replica_groups=mesh['dp'=16,'stream'=2] {'dp','stream'}, use_global_device_ids=true, to_apply=%region_14.0 | all-reduce | flops 3072 | bytes 12288 | tf_op jit(solution)/shard_map/psum | solution.py:294
  341.4 4.3 add_convert_fusion.3
  345.6 49.9 %all-reduce.5.cloned.1.call-done = (bf16[768,1536]{1,0:T(8,128)(2,1)}, bf16[768,768]{1,0:T(8,128)(2,1)}, bf16[768,768]{1,0:T(8,128)(2,1)}) async-done(((bf16[768,1536]{1,0:T(8,128)(2,1)}, bf16[768,768]{1,0:T(8,128)(2,1)}, bf16[768,768]{1,0:T(8,128)(2,1)}), (bf16[768,1536]{1,0:T(8,128)(2,1)}, bf16[768,768]{1,0:T(8,128)(2,1)}, bf16[768,768]{1,0:T(8,128)(2,1)})) %all-reduce.5.cloned.1.call-update) | async-done | bytes 4718608 | tf_op jit(solution)/shard_map/psum | solution.py:294
  395.5 3.0 convert_element_type.155
  398.5 3.4 maximum_convert_fusion
  402.0 181.7 %all-reduce.7.cloned.1.call-done = (bf16[1,768,3072]{2,1,0:T(8,128)(2,1)}, bf16[1,3072,768]{2,1,0:T(8,128)(2,1)}) async-done(((bf16[1,768,3072]{2,1,0:T(8,128)(2,1)}, bf16[1,3072,768]{2,1,0:T(8,128)(2,1)}), (bf16[1,768,3072]{2,1,0:T(8,128)(2,1)}, bf16[1,3072,768]{2,1,0:T(8,128)(2,1)})) %all-reduce.7.cloned.1.call-update) | async-done | bytes 9437200 | tf_op jit(solution)/shard_map/psum | solution.py:274
  583.7 7.5 %broadcast_in_dim.43 = f32[1,768,3072]{2,1,0:T(8,128)} convert(bf16[1,768,3072]{2,1,0:T(8,128)(2,1)} %get-tuple-element.57) | non-fusion elementwise | flops 2359296 | bytes 14155776 | tf_op jit(solution)/shard_map/broadcast_in_dim | solution.py:317
  591.3 4.5 broadcast_in_dim.45
  (130 shorter events, 24.5 us)
Async XLA Ops:
  7.2 68.2 %copy-start = (bf16[768,768]{1,0:T(8,128)(2,1)S(1)}, bf16[768,768]{1,0:T(8,128)(2,1)}, u32[]{:S(2)}) copy-start(bf16[768,768]{1,0:T(8,128)(2,1)} %param.18) | copy-start | bytes 3538948
  7.2 7.7 %copy-start.29 = (s32[5,200]{1,0:T(8,128)S(1)}, s32[5,200]{1,0:T(8,128)}, u32[]{:S(2)}) copy-start(s32[5,200]{1,0:T(8,128)} %param.14) | copy-start | bytes 12004
  7.2 7.9 %copy-start.34 = (f32[1,768]{1,0:T(1,128)S(1)}, f32[1,768]{1,0:T(1,128)}, u32[]{:S(2)}) copy-start(f32[1,768]{1,0:T(1,128)} %param.21) | copy-start | bytes 9220
  7.2 7.9 %copy-start.35 = (f32[1,768]{1,0:T(1,128)S(1)}, f32[1,768]{1,0:T(1,128)}, u32[]{:S(2)}) copy-start(f32[1,768]{1,0:T(1,128)} %param.22) | copy-start | bytes 9220
  7.2 7.9 %copy-start.33 = (f32[768]{0:T(1024)S(1)}, f32[768]{0:T(1024)}, u32[]{:S(2)}) copy-start(f32[768]{0:T(1024)} %param.20) | copy-start | bytes 9220
  7.2 388.3 %all-reduce.5.cloned.1.call-start = ((), (), s32[]{:S(2)}) async-start(), calls=%async_computation | async-start | bytes 9437184 | tf_op jit(solution)/shard_map/psum | solution.py:294
  7.3 10.9 %copy-start.6 = (bf16[5,1,200,768]{3,2,1,0:T(8,128)(2,1)S(1)}, bf16[5,1,200,768]{3,2,1,0:T(8,128)(2,1)}, u32[]{:S(2)}) copy-start(bf16[5,1,200,768]{3,2,1,0:T(8,128)(2,1)} %param.13) | copy-start | bytes 4608004
  7.3 10.9 %copy-start.17 = (f32[768]{0:T(1024)S(1)}, f32[768]{0:T(1024)}, u32[]{:S(2)}) copy-start(f32[768]{0:T(1024)} %param.16) | copy-start | bytes 9220
  7.3 10.9 %copy-start.19 = (f32[768]{0:T(1024)S(1)}, f32[768]{0:T(1024)}, u32[]{:S(2)}) copy-start(f32[768]{0:T(1024)} %param.15) | copy-start | bytes 9220
  7.3 37.0 %collective-permute-start = (bf16[1000,768]{1,0:T(8,128)(2,1)}, bf16[1000,768]{1,0:T(8,128)(2,1)}, u32[]{:S(2)}, u32[]{:S(2)}) collective-permute-start(bf16[1000,768]{1,0:T(8,128)(2,1)} %bitcast.88), channel_id=1, source_target_pairs={{0,1},{1,0},{2,3},{3,2},{4,5},{5,4},{6,7},{7,6},{8,9},{9,8},{10,11... | collective-permute-start | bytes 4608008 | tf_op jit(solution)/shard_map/ppermute | solution.py:240
  14.2 5.7 copy-start.21
  14.9 5.1 copy-start.23
  15.2 4.8 copy-start.36
  24.5 27.9 %copy-start.3 = (bf16[1000,2304]{1,0:T(8,128)(2,1)}, bf16[1000,2304]{1,0:T(8,128)(2,1)S(1)}, u32[]{:S(2)}) copy-start(bf16[1000,2304]{1,0:T(8,128)(2,1)S(1)} %convolution_convert_fusion) | copy-start | bytes 13824004
  46.0 6.3 %copy-start.25 = (f32[1000]{0:T(1024)}, f32[1000]{0:T(1024)S(1)}, u32[]{:S(2)}) copy-start(f32[1000]{0:T(1024)S(1)} %broadcast_multiply_fusion.2) | copy-start | bytes 12004
  52.3 23.0 %copy-start.4 = (bf16[1000,1536]{1,0:T(8,128)(2,1)}, bf16[1000,1536]{1,0:T(8,128)(2,1)S(1)}, u32[]{:S(2)}) copy-start(bf16[1000,1536]{1,0:T(8,128)(2,1)S(1)} %convolution_convert_fusion.3) | copy-start | bytes 9216004
  52.3 23.0 %copy-start.30 = (f32[768]{0:T(1024)S(1)}, f32[768]{0:T(1024)}, u32[]{:S(2)}) copy-start(f32[768]{0:T(1024)} %param.19) | copy-start | bytes 9220
  84.4 35.6 %copy-start.15 = (bf16[5,1,200,768]{3,2,1,0:T(8,128)(2,1)S(1)}, bf16[5,1,200,768]{3,2,1,0:T(8,128)(2,1)}, u32[]{:S(2)}) copy-start(bf16[5,1,200,768]{3,2,1,0:T(8,128)(2,1)} %fusion.33) | copy-start | bytes 4608004
  135.5 11.3 %copy-start.11 = (bf16[5,1,200,768]{3,2,1,0:T(8,128)(2,1)S(1)}, bf16[5,1,200,768]{3,2,1,0:T(8,128)(2,1)}, u32[]{:S(2)}) copy-start(bf16[5,1,200,768]{3,2,1,0:T(8,128)(2,1)} %param.25) | copy-start | bytes 4608004
  135.5 11.3 %copy-start.38 = (bf16[1000,3072]{1,0:T(8,128)(2,1)S(1)}, bf16[1000,3072]{1,0:T(8,128)(2,1)}, u32[]{:S(2)}) copy-start(bf16[1000,3072]{1,0:T(8,128)(2,1)} %get-tuple-element.63) | copy-start | bytes 18432004
  135.6 24.4 %slice-start = ((s8[4608000]{0:T(1024)(128)(4,1)}), s8[4194304]{0:T(1024)(128)(4,1)S(1)}, s32[]{:S(2)}) async-start(s8[4608000]{0:T(1024)(128)(4,1)} %bitcast.80), calls=%async_computation.2 | async-start | bytes 8388608
  146.8 11.0 %copy-start.9 = (f32[1000,768]{1,0:T(8,128)S(1)}, f32[1000,768]{1,0:T(8,128)}, u32[]{:S(2)}) copy-start(f32[1000,768]{1,0:T(8,128)} %get-tuple-element.79) | copy-start | bytes 9216004
  146.8 13.1 %slice-start.1 = ((s8[4608000]{0:T(1024)(128)(4,1)}), s8[413696]{0:T(1024)(128)(4,1)S(1)}, s32[]{:S(2)}) async-start(s8[4608000]{0:T(1024)(128)(4,1)} %bitcast.80), calls=%async_computation.3 | async-start | bytes 827392
  158.4 46.8 %copy-start.10 = (f32[1000,768]{1,0:T(8,128)}, f32[1000,768]{1,0:T(8,128)S(1)}, u32[]{:S(2)}) copy-start(f32[1000,768]{1,0:T(8,128)S(1)} %get-tuple-element.60) | copy-start | bytes 9216004
  197.6 4.4 copy-start.24
  200.2 34.8 %collective-permute-start.1 = (bf16[1000,768]{1,0:T(8,128)(2,1)S(1)}, bf16[1000,768]{1,0:T(8,128)(2,1)S(1)}, u32[]{:S(2)}, u32[]{:S(2)}) collective-permute-start(bf16[1000,768]{1,0:T(8,128)(2,1)S(1)} %fusion.41), channel_id=1, source_target_pairs={{0,1},{1,0},{2,3},{3,2},{4,5},{5,4},{6,7},{7,6},{8,9},{9,8},{10,11... | collective-permute-start | bytes 4608008 | tf_op jit(solution)/shard_map/ppermute | solution.py:285
  210.4 27.1 %copy-start.28 = (f32[1000]{0:T(1024)S(1)}, f32[1000]{0:T(1024)}, u32[]{:S(2)}) copy-start(f32[1000]{0:T(1024)} %copy-done.27) | copy-start | bytes 12004
  210.4 27.1 %copy-start.26 = (f32[1000]{0:T(1024)S(1)}, f32[1000]{0:T(1024)}, u32[]{:S(2)}) copy-start(f32[1000]{0:T(1024)} %copy-done.25) | copy-start | bytes 12004
  210.4 27.1 %copy-start.32 = (f32[1000]{0:T(1024)S(1)}, f32[1000]{0:T(1024)}, u32[]{:S(2)}) copy-start(f32[1000]{0:T(1024)} %copy-done.31) | copy-start | bytes 12004
  248.2 335.5 %all-reduce.7.cloned.1.call-start = ((), (), s32[]{:S(2)}) async-start(), calls=%async_computation.1 | async-start | bytes 18874368 | tf_op jit(solution)/shard_map/psum | solution.py:274
  248.3 10.4 %copy-start.39 = (bf16[1000,768]{1,0:T(8,128)(2,1)S(1)}, bf16[1000,768]{1,0:T(8,128)(2,1)}, u32[]{:S(2)}) copy-start(bf16[1000,768]{1,0:T(8,128)(2,1)} %get-tuple-element.71) | copy-start | bytes 4608004
  583.7 7.5 %copy-start.12 = (bf16[1,3072,768]{2,1,0:T(8,128)(2,1)S(1)}, bf16[1,3072,768]{2,1,0:T(8,128)(2,1)}, u32[]{:S(2)}) copy-start(bf16[1,3072,768]{2,1,0:T(8,128)(2,1)} %get-tuple-element.58) | copy-start | bytes 14155780
  (14 other events, 45.6 us)
Sparse Core Ops, SparseCore 0:
  248.4 147.1 all-reduce.4
  399.8 183.8 all-reduce.6

commit v2 on v1

--- a/solution.py
+++ b/solution.py
@@ -19,11 +19,19 @@
 BF16 = jnp.bfloat16
 
 
-def layer_norm(inputs, gain_row, bias_row):
+def normalized(inputs):
     row_mean = jnp.mean(inputs, axis=-1, keepdims=True)
     centered = inputs - row_mean
     variance = jnp.mean(centered * centered, axis=-1, keepdims=True)
-    return centered * lax.rsqrt(variance + EPSILON) * gain_row + bias_row
+    inverse = lax.rsqrt(variance + EPSILON)
+    return centered * inverse, inverse
+
+
+def norm_input_grad(normed, inverse, gain_row, grad):
+    scaled = grad * gain_row
+    mean_scaled = jnp.mean(scaled, axis=-1, keepdims=True)
+    mean_product = jnp.mean(scaled * normed, axis=-1, keepdims=True)
+    return inverse * (scaled - mean_scaled - normed * mean_product)
 
 
 def gelu_exact(inputs):
@@ -215,7 +223,364 @@
     )(stream, seg_row, seg_col, qkv, other, g_mix, lse)
 
 
+class Plan:
+    def __init__(self, dp, streams):
+        self.outer = 4
+        self.inner = max(dp // 8, 1)
+        self.dp = dp
+        self.streams = streams
+
+    def pieces(self, partials):
+        if self.dp != 2 * self.outer * self.inner:
+            return None
+        pieces = []
+        for array, shared, cuts in zip(partials, SHARED, CUTS):
+            piece = array.shape[0] // cuts
+            parts = self.inner * self.outer * (self.streams if shared else 1)
+            if array.shape[0] % cuts or piece % (16 * parts) or array.shape[1] % (2 * LANES):
+                return None
+            pieces.append(piece)
+        return pieces
+
+
+def add_rows(target, first, others, rows):
+    step = 16
+    for candidate in (64, 48, 32):
+        if rows % candidate == 0:
+            step = candidate
+            break
+
+    def band(i, carry):
+        at = pl.ds(pl.multiple_of(i * step, step), step)
+        total = first[at, :].astype(F32)
+        for ref in others:
+            total = total + ref[at, :].astype(F32)
+        target[at, :] = total.astype(target.dtype)
+        return carry
+
+    lax.fori_loop(0, rows // step, band, 0)
+
+
+def job_levels(plan, shared):
+    levels = [("inner", plan.inner), ("outer", plan.outer)]
+    return ([("stream", plan.streams)] if shared else []) + levels
+
+
+def job_scratch(plan, job):
+    rows, half, shared = job[2], job[3] // 2, job[4]
+    shapes = [pltpu.VMEM((rows, half), BF16), pltpu.VMEM((rows, half), BF16)]
+    for _, size in job_levels(plan, shared):
+        rows = rows // size
+        shapes.append(pltpu.VMEM((size - 1, rows, half), BF16))
+        shapes.append(pltpu.VMEM((rows, half), BF16))
+    copies = 2 + 2 * sum(size - 1 for _, size in job_levels(plan, shared))
+    shapes += [
+        pltpu.SemaphoreType.DMA((copies,)),
+        pltpu.SemaphoreType.DMA((copies,)),
+        pltpu.SemaphoreType.DMA((2,)),
+    ]
+    return shapes
+
+
+def reduce_kernel(plan, jobs, count, *refs):
+    ins, small_in = refs[:count], refs[count]
+    outs, small_out = refs[count + 1 : 2 * count + 1], refs[2 * count + 1]
+    scratch = list(refs[2 * count + 2 :])
+    dp_index, stream_index = lax.axis_index("dp"), lax.axis_index("stream")
+    place = {
+        "core": dp_index % 2,
+        "inner": (dp_index // 2) % plan.inner,
+        "outer": dp_index // (2 * plan.inner),
+        "stream": stream_index,
+    }
+    sizes = {"core": 2, "inner": plan.inner, "outer": plan.outer, "stream": plan.streams}
+
+    def peer(axis, offset):
+        at = dict(place)
+        at[axis] = (place[axis] + offset) % sizes[axis]
+        dp = (at["outer"] * plan.inner + at["inner"]) * 2 + at["core"]
+        return (dp, at["stream"]), at[axis]
+
+    barrier = pltpu.get_barrier_semaphore()
+    neighbours = [peer(axis, o)[0] for axis in sizes for o in range(1, sizes[axis])]
+    for device in neighbours:
+        pl.semaphore_signal(barrier, inc=1, device_id=device, device_id_type=pl.DeviceIdType.MESH)
+    pl.semaphore_wait(barrier, len(neighbours))
+    sent = []
+
+    def send(source, target, send_sem, recv_sem, device):
+        copy = pltpu.make_async_remote_copy(
+            src_ref=source,
+            dst_ref=target,
+            send_sem=send_sem,
+            recv_sem=recv_sem,
+            device_id=device,
+            device_id_type=pl.DeviceIdType.MESH,
+        )
+        copy.start()
+        sent.append(copy)
+        return copy
+
+    def job_stages(job):
+        array, start, rows, columns, shared = job
+        half = columns // 2
+        levels = job_levels(plan, shared)
+        mine, partner = scratch.pop(0), scratch.pop(0)
+        stages_refs = [(scratch.pop(0), scratch.pop(0)) for _ in levels]
+        send_sems, recv_sems, local_sems = scratch.pop(0), scratch.pop(0), scratch.pop(0)
+        source, result = ins[array], outs[array]
+        own_columns = pl.ds(pl.multiple_of(place["core"] * half, half), half)
+        far_columns = pl.ds(pl.multiple_of((1 - place["core"]) * half, half), half)
+        state = {"slot": 0}
+        waits = {}
+
+        def next_slot():
+            state["slot"] += 1
+            return state["slot"] - 1
+
+        def begin():
+            slot = next_slot()
+            device, _ = peer("core", 1)
+            waits["core"] = send(
+                source.at[pl.ds(start, rows), far_columns], partner, send_sems.at[slot], recv_sems.at[slot], device
+            )
+            waits["local"] = pltpu.make_async_copy(
+                source.at[pl.ds(start, rows), own_columns], mine, local_sems.at[0]
+            )
+            waits["local"].start()
+
+        def spread(index, held, held_rows):
+            axis, size = levels[index]
+            part = held_rows // size
+            waits[index] = []
+            for offset in range(1, size):
+                slot = next_slot()
+                device, target = peer(axis, offset)
+                rows_at = pl.ds(pl.multiple_of(target * part, part), part)
+                waits[index].append(
+                    send(
+                        held.at[rows_at, :],
+                        stages_refs[index][0].at[offset - 1],
+                        send_sems.at[slot],
+                        recv_sems.at[slot],
+                        device,
+                    )
+                )
+
+        def first_sum():
+            waits["local"].wait()
+            waits["core"].wait_recv()
+            add_rows(mine, mine, [partner], rows)
+            spread(0, mine, rows)
+
+        def held_before(index):
+            return (mine, rows) if index == 0 else (stages_refs[index - 1][1], rows_before[index])
+
+        rows_before = [rows]
+        for _, size in levels:
+            rows_before.append(rows_before[-1] // size)
+
+        def level_sum(index):
+            axis, size = levels[index]
+            held = held_before(index)[0]
+            part = rows_before[index + 1]
+            received, total = stages_refs[index]
+            for copy in waits[index]:
+                copy.wait_recv()
+            own = held.at[pl.ds(pl.multiple_of(place[axis] * part, part), part), :]
+            add_rows(total, own, [received.at[o] for o in range(size - 1)], part)
+
+        def gathered(index):
+            offset = start
+            for level in range(index):
+                offset = offset + place[levels[level][0]] * rows_before[level + 1]
+            return pl.ds(pl.multiple_of(offset, 16), rows_before[index])
+
+        def gather(index, held):
+            axis, size = levels[index]
+            region = result.at[gathered(index + 1), own_columns]
+            waits[("gather", index)] = []
+            for offset in range(1, size):
+                slot = next_slot()
+                device, _ = peer(axis, offset)
+                waits[("gather", index)].append(
+                    send(held if held is not None else region, region, send_sems.at[slot], recv_sems.at[slot], device)
+                )
+
+        def wait_gather(index):
+            for copy in waits[("gather", index)]:
+                copy.wait_recv()
+
+        last = len(levels) - 1
+        stages = [begin, first_sum]
+        for index in range(last):
+            def middle(index=index):
+                level_sum(index)
+                spread(index + 1, stages_refs[index][1], rows_before[index + 1])
+            stages.append(middle)
+
+        def turn():
+            level_sum(last)
+            total = stages_refs[last][1]
+            gather(last, total)
+            waits["out"] = pltpu.make_async_copy(
+                total, result.at[gathered(last + 1), own_columns], local_sems.at[1]
+            )
+            waits["out"].start()
+
+        stages.append(turn)
+        for index in range(last, 0, -1):
+            def up(index=index):
+                wait_gather(index)
+                if index == last:
+                    waits["out"].wait()
+                gather(index - 1, None)
+            stages.append(up)
+
+        def core_gather():
+            wait_gather(0)
+            slot = next_slot()
+            device, _ = peer("core", 1)
+            region = result.at[pl.ds(start, rows), own_columns]
+            waits["back"] = send(region, region, send_sems.at[slot], recv_sems.at[slot], device)
+
+        def finish():
+            waits["back"].wait_recv()
+
+        return stages + [core_gather, finish]
+
+    def small_stages():
+        rows, columns = small_in.shape
+        order = ["core", "stream", "inner", "outer"]
+        held = [scratch.pop(0) for _ in order]
+        own, local = scratch.pop(0), scratch.pop(0)
+        send_sems, recv_sems = scratch.pop(0), scratch.pop(0)
+        slot = 0
+        stages = []
+        plans = []
+        for axis in order:
+            plans.append((axis, [slot + i for i in range(sizes[axis] - 1)]))
+            slot += sizes[axis] - 1
+        pending = {}
+
+        def share(index, value_ref):
+            axis, slots = plans[index]
+            pending[index] = []
+            for offset, at in enumerate(slots, 1):
+                device, _ = peer(axis, offset)
+                pending[index].append(
+                    send(value_ref, held[index].at[offset - 1], send_sems.at[at], recv_sems.at[at], device)
+                )
+
+        def collect(index, value_ref):
+            axis, _ = plans[index]
+            size = sizes[axis]
+            for copy in pending[index]:
+                copy.wait_recv()
+            total = None
+            for member in range(size):
+                term = jnp.where(place[axis] == member, value_ref[...], jnp.zeros(value_ref.shape, F32))
+                for offset in range(1, size):
+                    is_there = (member + offset) % size == place[axis]
+                    term = term + jnp.where(is_there, held[index][offset - 1], jnp.zeros(value_ref.shape, F32))
+                total = term if total is None else total + term
+            return total
+
+        def begin():
+            share(0, small_in)
+
+        def step(index):
+            value_ref = small_in if index == 0 else own.at[index - 1]
+            own[index] = collect(index, value_ref)
+            share(index + 1, own.at[index])
+
+        def finish():
+            small_out[...] = collect(len(order) - 1, own.at[len(order) - 2])
+
+        stages = [begin]
+        for index in range(len(order) - 1):
+            stages.append(functools.partial(step, index))
+        return stages + [finish]
+
+    pipelines = [job_stages(job) for job in jobs]
+    small = small_stages()
+    small[0]()
+    for stages in pipelines:
+        stages[0]()
+    starts = [0] * len(pipelines)
+    tick = {False: 0, True: 0}
+    for i, job in enumerate(jobs):
+        starts[i] = tick[job[4]]
+        tick[job[4]] += 1
+    last_tick = max(s + len(p) for s, p in zip(starts, pipelines))
+    for now in range(last_tick):
+        for begin_at, stages in zip(starts, pipelines):
+            at = now - begin_at + 1
+            if 1 <= at < len(stages):
+                stages[at]()
+        if 1 <= now + 1 < len(small):
+            small[now + 1]()
+    for copy in sent:
+        copy.wait_send()
+
+
+def reduce_jobs(arrays, shared_flags, pieces):
+    expert, common = [], []
+    for index, (array, shared, piece) in enumerate(zip(arrays, shared_flags, pieces)):
+        rows, columns = array.shape
+        for start in range(0, rows, piece):
+            (common if shared else expert).append((index, start, piece, columns, shared))
+    merged = []
+    while expert or common:
+        if expert:
+            merged.append(expert.pop(0))
+        if common:
+            merged.append(common.pop(0))
+    return merged
+
+
+def reduce_all(plan, arrays, shared_flags, pieces, small):
+    jobs = reduce_jobs(arrays, shared_flags, pieces)
+    scratch = []
+    for job in jobs:
+        scratch += job_scratch(plan, job)
+    small_shape = small.shape
+    sizes = [2, plan.streams, plan.inner, plan.outer]
+    scratch += [pltpu.VMEM((max(size - 1, 1),) + small_shape, F32) for size in sizes]
+    scratch += [pltpu.VMEM((4,) + small_shape, F32), pltpu.VMEM(small_shape, F32)]
+    copies = sum(size - 1 for size in sizes)
+    scratch += [pltpu.SemaphoreType.DMA((copies,)), pltpu.SemaphoreType.DMA((copies,))]
+    anywhere = pl.BlockSpec(memory_space=pl.ANY)
+    in_vmem = pl.BlockSpec(memory_space=pltpu.VMEM)
+    result = pl.pallas_call(
+        functools.partial(reduce_kernel, plan, jobs, len(arrays)),
+        in_specs=[anywhere] * len(arrays) + [in_vmem],
+        out_specs=[anywhere] * len(arrays) + [in_vmem],
+        out_shape=[jax.ShapeDtypeStruct(a.shape, a.dtype) for a in arrays]
+        + [jax.ShapeDtypeStruct(small_shape, F32)],
+        scratch_shapes=scratch,
+        compiler_params=pltpu.CompilerParams(
+            collective_id=0, has_side_effects=True, vmem_limit_bytes=56 << 20
+        ),
+        name="reduce_all",
+    )(*arrays, small)
+    return result[:-1], result[-1]
+
+SHARED = (False, False, True, True, True)
+CUTS = (3, 3, 3, 1, 1)
+
+
+def reduce_partials(plan, partials, small):
+    pieces = plan.pieces(partials)
+    if pieces is not None:
+        return reduce_all(plan, partials, SHARED, pieces, small)
+    everyone = ("dp", "stream")
+    totals = [lax.psum(p, everyone if shared else "dp") for p, shared in zip(partials, SHARED)]
+    return totals, lax.psum(small, everyone)
+
+
 def shards(
+    plan,
     tokens,
     text_segment,
     ln1_gain,
@@ -239,10 +604,11 @@
     own_tokens = tokens.reshape(rows, width)
     other_tokens = lax.ppermute(own_tokens, "stream", swap)
     flat_rows = own_tokens.astype(F32)
-    attn_in, ln1_pull = jax.vjp(layer_norm, flat_rows, ln1_gain, ln1_bias)
-    attn_low = attn_in.astype(BF16)
+    normed, inverse = normalized(flat_rows)
+    attn_low = (normed * ln1_gain + ln1_bias).astype(BF16)
     qkv = dot_nn(attn_low, qkv_weight).astype(BF16)
-    other_low = layer_norm(other_tokens.astype(F32), ln1_gain, ln1_bias).astype(BF16)
+    other_normed, _ = normalized(other_tokens.astype(F32))
+    other_low = (other_normed * ln1_gain + ln1_bias).astype(BF16)
     kv_weight = qkv_weight[:, width:]
     other_kv = dot_nn(other_low, kv_weight).astype(BF16)
     qkv = qkv.reshape(groups, slots, 3 * width)
@@ -253,8 +619,8 @@
     residual = flat_rows + attn_scale * attn_proj
     in_matrix = expert_in[0]
     out_matrix = expert_out[0]
-    ffn_in, ln2_pull = jax.vjp(layer_norm, residual, ln2_gain[0], ln2_bias[0])
-    ffn_low = ffn_in.astype(BF16)
+    normed2, inverse2 = normalized(residual)
+    ffn_low = (normed2 * ln2_gain[0] + ln2_bias[0]).astype(BF16)
     pre_act = dot_nn(ffn_low, in_matrix)
     activation = gelu_exact(pre_act).astype(BF16)
     ffn_out = dot_nn(activation, out_matrix)
@@ -268,12 +634,9 @@
     grad_pre = gelu_pull(grad_act)[0].astype(BF16)
     expert_in_grad = dot_tn(ffn_low, grad_pre)
     grad_ffn_in = dot_nt(grad_pre, in_matrix)
-    grad_resid_norm, ln2_gain_grad, ln2_bias_grad = ln2_pull(grad_ffn_in)
-    grad_resid = grad_out + grad_resid_norm
-    small_expert = jnp.stack([ln2_gain_grad, ln2_bias_grad], axis=0)
-    expert_total = lax.psum(
-        (expert_in_grad.astype(BF16), expert_out_grad.astype(BF16), small_expert.astype(BF16)), "dp"
-    )
+    ln2_gain_grad = jnp.sum(grad_ffn_in * normed2, axis=0)
+    ln2_bias_grad = jnp.sum(grad_ffn_in, axis=0)
+    grad_resid = grad_out + norm_input_grad(normed2, inverse2, ln2_gain[0], grad_ffn_in)
     attn_scale_grad = jnp.sum(grad_resid * attn_proj, axis=0)
     grad_proj = (attn_scale * grad_resid).astype(BF16)
     out_weight_grad = dot_tn(mixed, grad_proj)
@@ -281,41 +644,50 @@
     grad_query, grad_kv = attend_back(stream, seg_row, seg_col, qkv, other_kv, grad_mix, lse)
     grad_query = grad_query.reshape(rows, width)
     grad_kv = grad_kv.reshape(2, rows, 2 * width)
-    back = dot_nt(grad_kv[1], kv_weight).astype(BF16)
-    returned = lax.ppermute(back, "stream", swap)
+    other_back = dot_nt(grad_kv[1], kv_weight)
+    returned = lax.ppermute(other_back.astype(BF16), "stream", swap)
     query_weight_grad = dot_tn(attn_low, grad_query)
     both_low = jnp.stack([attn_low, other_low], axis=0).reshape(2 * rows, width)
     kv_weight_grad = dot_tn(both_low, grad_kv.reshape(2 * rows, 2 * width))
     own_back = dot_nt(grad_query, qkv_weight[:, :width]) + dot_nt(grad_kv[0], kv_weight)
+    ln1_gain_grad = jnp.sum(own_back * normed, axis=0) + jnp.sum(other_back * other_normed, axis=0)
+    ln1_bias_grad = jnp.sum(own_back, axis=0) + jnp.sum(other_back, axis=0)
+    here = lax.broadcasted_iota(jnp.int32, (plan.streams, 1), 0) == stream
+    small = jnp.concatenate(
+        [
+            jnp.stack([ln1_gain_grad, ln1_bias_grad, attn_scale_grad, ffn_scale_grad], axis=0),
+            jnp.where(here, ln2_gain_grad[None], 0.0),
+            jnp.where(here, ln2_bias_grad[None], 0.0),
+        ],
+        axis=0,
+    )
+    partials = [
+        expert_in_grad.astype(BF16),
+        expert_out_grad.astype(BF16),
+        kv_weight_grad.astype(BF16),
+        query_weight_grad.astype(BF16),
+        out_weight_grad.astype(BF16),
+    ]
+    totals, small_total = reduce_partials(plan, partials, small)
     grad_attn_in = own_back + returned.astype(F32)
-    grad_rows_norm, ln1_gain_grad, ln1_bias_grad = ln1_pull(grad_attn_in)
+    grad_rows_norm = norm_input_grad(normed, inverse, ln1_gain, grad_attn_in)
     tokens_grad = (grad_resid + grad_rows_norm).astype(BF16).reshape(tokens.shape)
-    small_grads = jnp.stack([ln1_gain_grad, ln1_bias_grad, attn_scale_grad, ffn_scale_grad], axis=0)
-    shared_total = lax.psum(
-        (
-            query_weight_grad.astype(BF16),
-            kv_weight_grad.astype(BF16),
-            out_weight_grad.astype(BF16),
-            small_grads.astype(BF16),
-        ),
-        ("dp", "stream"),
-    )
-    small_total = shared_total[3].astype(F32)
-    small_expert = expert_total[2].astype(F32)
-    qkv_weight_grad = jnp.concatenate([shared_total[0], shared_total[1]], axis=1).astype(F32)
+    expert_in_total, expert_out_total, kv_total, query_total, out_total = totals
+    ln2_gain_total = jnp.sum(jnp.where(here, small_total[4 : 4 + plan.streams], 0.0), axis=0)
+    ln2_bias_total = jnp.sum(jnp.where(here, small_total[4 + plan.streams :], 0.0), axis=0)
     return (
         block_out.reshape(tokens.shape),
         tokens_grad,
         small_total[0],
         small_total[1],
-        qkv_weight_grad,
-        shared_total[2].astype(F32),
+        jnp.concatenate([query_total, kv_total], axis=1).astype(F32),
+        out_total.astype(F32),
         small_total[2],
         small_total[3],
-        small_expert[0][None, :],
-        small_expert[1][None, :],
-        expert_total[0].astype(F32)[None],
-        expert_total[1].astype(F32)[None],
+        ln2_gain_total[None],
+        ln2_bias_total[None],
+        expert_in_total.astype(F32)[None],
+        expert_out_total.astype(F32)[None],
     )
 
 
@@ -350,4 +722,5 @@
         P("stream", None, None),
         P("stream", None, None),
     )
-    return jax.shard_map(shards, mesh=mesh, in_specs=ins, out_specs=outs, check_vma=False)
+    plan = Plan(mesh.shape["dp"], mesh.shape["stream"])
+    return jax.shard_map(functools.partial(shards, plan), mesh=mesh, in_specs=ins, out_specs=outs, check_vma=False)

time: 610 us -> 441 us (0.72)
  waiting for transfers between devices: 276 us -> 21.5 us
  Pallas kernels: 57.1 us -> 228 us
  blocking collectives: 69 us -> 0 us
  between operations: 15.2 us -> 1.72 us
    psum x2 -> x0, waiting for transfers between devices: 232 us -> none  [the longest x1 182 us: shards(): lax.psum((expert_in_grad.astype(BF16), expert_out_grad.astype(BF16), smal...]
    pallas_call x0 -> x1, Pallas kernels: none -> 171 us  [reduce_all(): pl.pallas_call(functools.partial(reduce_kernel, plan, jobs, len(arrays)),...]
    psum x2 -> x0, blocking collectives: 69 us -> none  [the longest x1 37.1 us: shards(): lax.psum((query_weight_grad.astype(BF16), kv_weight_grad.astype(BF16), ou...]
    ppermute x1, waiting for transfers between devices: 24.6 us -> 3.32 us  [shards(): returned = lax.ppermute(other_back.astype(BF16), 'stream', swap)]
    reduce_sum x8 -> x7, other arithmetic: 14.6 us -> 12.9 us  [the longest x3 6.44 us: normalized(): variance = jnp.mean(centered * centered, axis=-1, keepdims=True)]
  transfers between devices with their start and end apart: 4 -> 2, of which waited for: 4 -> 2; matrix products, arithmetic and copies ran while one was open for 9% -> 10% of each run, Pallas kernels for 0% -> 0%
where the time goes in v2:
time: 441 us; the launch traced here: 434 us
  Pallas kernels  228 us (52%)
  matrix products  127 us (29%)
  other arithmetic  41.4 us (9%)
  waiting for transfers between devices  21.5 us (5%)
  local copies, waits for them, and re-layouts  8.81 us (2%)
  starting transfers between devices  4.86 us (1%)
    pallas_call x1, Pallas kernels, reduce_all(): pl.pallas_call(functools.partial(reduce_kernel, plan, jobs, len(arrays)),...  171 us
    dot_general x5, matrix products, dot_nn(): lax.dot_general(a, b, (((1,), (0,)), ((), ())), preferred_element_type=F32)  60.2 us
    dot_general x6, matrix products, dot_nt(): lax.dot_general(a, b, (((1,), (1,)), ((), ())), preferred_element_type=F32)  37.9 us
    pallas_call x1, Pallas kernels, attend_back(): pl.pallas_call(attend_back_kernel, grid=(groups,), in_specs=attention_spe...  33.9 us
    dot_general x5, matrix products, dot_tn(): lax.dot_general(a, b, (((0,), (0,)), ((), ())), preferred_element_type=F32)  29.1 us
    pallas_call x1, Pallas kernels, attend(): pl.pallas_call(attend_kernel, grid=(groups,), in_specs=attention_specs(sl...  23 us
    ppermute x1, waiting for transfers between devices, shards(): other_tokens = lax.ppermute(own_tokens, 'stream', swap)  18.2 us
  transfers between devices with their start and end apart: 2, of which 2 were waited for; matrix products, arithmetic and copies ran while one was open for 10% of the time, Pallas kernels for 0%

profile of v2, /device:TPU:0, one launch (start us, length us, event | category | flops | bytes accessed | tf_op | source)
XLA Modules:
  0.0 433.7 jit_solution(2055766784929488539)
XLA Ops:
  0.7 3.1 collective-permute-start
  5.6 2.0 multiply_reduce_fusion.4
  8.1 2.8 fusion.37
  14.9 4.5 %convolution_convert_fusion = bf16[1000,2304]{1,0:T(8,128)(2,1)S(1)} fusion(bf16[768,2304]{1,0:T(8,128)(2,1)S(1)} %copy-done.38, bf16[1000,768]{1,0:T(8,128)(2,1)S(1)} %bitcast.92, f32[768]{0:T(1024)S(1)} %copy-done.28, f32[768]{0:T(1024)S(1)} %copy-done.20, f32[1000]{0:T(1024)S(1)} %rsqrt.29, f32[1000]{0:T(1024)S(1)} %div.33), kind=kOutput, calls=%fused_computation.17 | convolution fusion | flops 3545856000 | bytes 9697088 | tf_op jit(solution)/shard_map/dot_general | solution.py:42
  19.5 18.2 %collective-permute-done = bf16[1000,768]{1,0:T(8,128)(2,1)} collective-permute-done((bf16[1000,768]{1,0:T(8,128)(2,1)}, bf16[1000,768]{1,0:T(8,128)(2,1)}, u32[]{:S(2)}, u32[]{:S(2)}) %collective-permute-start) | collective-permute-done | bytes 1536032 | tf_op jit(solution)/shard_map/ppermute | solution.py:605
  39.4 2.0 fusion.23
  41.4 4.3 convolution_convert_fusion.3
  45.7 23.0 %attend.1 = (bf16[5,200,768]{2,1,0:T(8,128)(2,1)S(1)}, f32[5,16,200]{2,1,0:T(8,128)S(1)}) custom-call(s32[1]{0:T(128)} %bitcast.1.stream_ref, s32[5,1,200]{2,1,0:T(1,128)S(1)} %reshape.319.seg_row_ref, s32[5,200,1]{2,1,0:T(8,128)S(1)} %copy.27.seg_col_ref, bf16[5,200,2304]{2,1,0:T(8,128)(2,1)S(1)} %bitcast.81, bf16[5,200,1536]{2,1,0:T(8,128)(2,1)S(1)} %bitcast.85), custom_call_target="tpu_custom_call" | custom-call | flops 1228800000 | bytes 9216000 | tf_op jit(solution)/shard_map/attend/pallas_call | solution.py:173
  68.8 4.1 convert_add_fusion
  72.9 2.1 reduce_sum.184
  75.0 2.5 multiply_reduce_fusion.3
  77.8 35.6 %multiply_convert_fusion = (bf16[1000,3072]{1,0:T(8,128)(2,1)}, f32[1000,3072]{1,0:T(8,128)}, f32[1000,3072]{1,0:T(8,128)}) fusion(bf16[1,768,3072]{2,1,0:T(8,128)(2,1)} %param.23, f32[1000,768]{1,0:T(8,128)S(1)} %copy-done.7, f32[768]{0:T(1024)S(1)} %reduce.5, f32[768]{0:T(1024)S(1)} %reduce.4, f32[1000]{0:T(1024)S(1)} %add_rsqrt_fusion.1, ...), kind=kOutput, calls=%fused_computation.3 | convolution fusion | flops 4922112000 | bytes 38524736 | tf_op jit(solution)/shard_map/dot_general | solution.py:42
  113.3 15.4 %add_convert_fusion = bf16[1000,3072]{1,0:T(8,128)(2,1)} fusion(f32[1000,3072]{1,0:T(8,128)} %get-tuple-element.75, f32[1000,3072]{1,0:T(8,128)} %get-tuple-element.89, bf16[1000,768]{1,0:T(8,128)(2,1)S(1)} %bitcast.101, bf16[1,3072,768]{2,1,0:T(8,128)(2,1)} %param.24), kind=kOutput, calls=%fused_computation.2 | convolution fusion | flops 4761600000 | bytes 36974592 | tf_op jit(solution)/shard_map/dot_general | solution.py:46
  128.7 9.9 %multiply_reduce_fusion = (f32[768]{0:T(1024)S(1)}, f32[1000]{0:T(1024)S(1)}, f32[1000]{0:T(1024)S(1)}, f32[768]{0:T(1024)S(1)}, f32[1000,768]{1,0:T(8,128)S(1)}) fusion(f32[1000,768]{1,0:T(8,128)S(1)} %copy-done.7, f32[1000]{0:T(1024)S(1)} %add_rsqrt_fusion.1, f32[1000]{0:T(1024)S(1)} %broadcast_multiply_fusion.5, f32[768]{0:T(1024)S(1)} %reduce.4, ...), kind=kOutput, calls=%fused_computation.66 | convolution fusion | flops 4725499904 | bytes 17031808 | tf_op jit(solution)/shard_map/dot_general | solution.py:46
  138.6 11.7 %fusion.39 = (f32[768]{0:T(1024)S(1)}, bf16[1000,768]{1,0:T(8,128)(2,1)}, f32[768]{0:T(1024)S(1)}, f32[1000,768]{1,0:T(8,128)S(1)}, bf16[1000,768]{1,0:T(8,128)(2,1)}) fusion(bf16[5,1,200,768]{3,2,1,0:T(8,128)(2,1)S(1)} %copy-done.16, f32[1000,768]{1,0:T(8,128)S(1)} %copy-done.7, f32[768]{0:T(1024)S(1)} %copy-done.32, f32[1000,768]{1,0:T(8,128)S(1)} %copy-done.8, ...), kind=kOutput, calls=%fused_computation.65 | convolution fusion | flops 4732413952 | bytes 27786880 | tf_op jit(solution)/shard_map/dot_general | solution.py:42
  152.0 2.5 convolution_convert_fusion.6.refs_4_
  155.3 33.9 %attend_back.1 = (bf16[5,200,768]{2,1,0:T(8,128)(2,1)S(1)}, bf16[2,5,200,1536]{3,2,1,0:T(8,128)(2,1)S(1)}) custom-call(s32[1]{0:T(128)} %bitcast.1.stream_ref, s32[5,1,200]{2,1,0:T(1,128)S(1)} %reshape.319.seg_row_ref, s32[5,200,1]{2,1,0:T(8,128)S(1)} %copy.27.seg_col_ref, bf16[5,200,2304]{2,1,0:T(8,128)(2,1)S(1)} %bitcast.84, ...), custom_call_target="tpu_custom_call" | custom-call | flops 3072000000 | bytes 18432000 | tf_op jit(solution)/shard_map/attend_back/pallas_call | solution.py:199
  191.3 4.4 %fusion.54 = (f32[768]{0:T(1024)S(1)}, f32[768]{0:T(1024)S(1)}, bf16[1000,768]{1,0:T(8,128)(2,1)S(1)}, bf16[1,1000,768]{2,1,0:T(8,128)(2,1)S(1)}) fusion(f32[1000]{0:T(1024)S(1)} %copy-done.34, f32[1000]{0:T(1024)S(1)} %copy-done.31, bf16[1000,768]{1,0:T(8,128)(2,1)} %collective-permute-done, f32[768]{0:T(1024)S(1)} %copy-done.29, f32[768]{0:T(1024)S(1)} %copy-done.21, ...), kind=kOutput, calls=%fused_computation.115 | convolution fusion | flops 2366974464 | bytes 10061824 | tf_op jit(solution)/shard_map/dot_general | solution.py:46
  195.8 1.8 collective-permute-start.1
  197.6 2.6 fusion.42
  200.2 10.1 %convolution_convert_fusion.1.refs_1_ = bf16[3072,768]{1,0:T(8,128)(2,1)} fusion(bf16[1000,3072]{1,0:T(8,128)(2,1)} %get-tuple-element.74, bf16[1000,768]{1,0:T(8,128)(2,1)S(1)} %copy-done.40), kind=kOutput, calls=%fused_computation.18 | convolution fusion | flops 4720951296 | bytes 12398592 | tf_op jit(solution)/shard_map/dot_general | solution.py:50
  210.7 6.5 %convolution_convert_fusion.4.refs_2_ = bf16[768,1536]{1,0:T(8,128)(2,1)} fusion(bf16[2000,768]{1,0:T(8,128)(2,1)S(1)} %bitcast.98, bf16[2000,1536]{1,0:T(8,128)(2,1)S(1)} %bitcast.78), kind=kOutput, calls=%fused_computation.40 | convolution fusion | flops 4719771648 | bytes 11575296 | tf_op jit(solution)/shard_map/dot_general | solution.py:50
  217.2 2.5 convolution_convert_fusion.7.refs_3_
  219.9 7.4 %convolution_convert_fusion.2.refs_0_ = bf16[768,3072]{1,0:T(8,128)(2,1)} fusion(bf16[1000,3072]{1,0:T(8,128)(2,1)S(1)} %bitcast.105, f32[1000,768]{1,0:T(8,128)S(1)} %copy-done.7, f32[768]{0:T(1024)S(1)} %reduce.5, f32[768]{0:T(1024)S(1)} %reduce.4, f32[1000]{0:T(1024)S(1)} %add_rsqrt_fusion.1, f32[1000]{0:T(1024)S(1)} %broadcast_multiply_fusion.5), kind=kOutput, calls=%fused_computation.19 | convolution fusion | flops 4724791296 | bytes 13948736 | tf_op jit(solution)/shard_map/dot_general | solution.py:50
  227.3 3.3 collective-permute-done.1
  230.6 4.2 fusion.51
  235.5 171.1 %reduce_all.1 = (bf16[768,3072]{1,0:T(8,128)(2,1)}, bf16[3072,768]{1,0:T(8,128)(2,1)}, bf16[768,1536]{1,0:T(8,128)(2,1)}, bf16[768,768]{1,0:T(8,128)(2,1)}, bf16[768,768]{1,0:T(8,128)(2,1)}, /*index=5*/f32[8,768]{1,0:T(8,128)}) custom-call(bf16[768,3072]{1,0:T(8,128)(2,1)} %convolution_convert_fusion.2.refs_0_, ...), custom_call_target="tpu_custom_call" | custom-call | tf_op jit(solution)/shard_map/reduce_all/pallas_call | solution.py:555
  409.1 3.0 convert_element_type.149
  413.2 7.4 %bitcast_convert_fusion.1 = f32[1,768,3072]{2,1,0:T(8,128)} fusion(bf16[768,3072]{1,0:T(8,128)(2,1)} %get-tuple-element.30), kind=kLoop, calls=%fused_computation.21 | loop fusion | flops 2359296 | bytes 14155776 | tf_op jit(solution)/shard_map/broadcast_in_dim | solution.py:689
  420.7 4.5 %bitcast_convert_fusion = f32[1,3072,768]{2,1,0:T(8,128)} fusion(bf16[3072,768]{1,0:T(8,128)(2,1)S(1)} %bitcast.95), kind=kLoop, calls=%fused_computation.20 | loop fusion | flops 2359296 | bytes 14155776 | tf_op jit(solution)/shard_map/broadcast_in_dim | solution.py:690
  425.2 4.1 maximum_convert_fusion
  430.9 2.3 fusion.35
  (132 shorter events, 19.1 us)
Async XLA Ops:
  0.6 68.1 %copy-start = (bf16[768,768]{1,0:T(8,128)(2,1)S(1)}, bf16[768,768]{1,0:T(8,128)(2,1)}, u32[]{:S(2)}) copy-start(bf16[768,768]{1,0:T(8,128)(2,1)} %param.18) | copy-start | bytes 3538948
  0.7 7.0 %copy-start.26 = (s32[5,200]{1,0:T(8,128)S(1)}, s32[5,200]{1,0:T(8,128)}, u32[]{:S(2)}) copy-start(s32[5,200]{1,0:T(8,128)} %param.14) | copy-start | bytes 12004
  0.7 7.3 %copy-start.35 = (f32[1,768]{1,0:T(1,128)S(1)}, f32[1,768]{1,0:T(1,128)}, u32[]{:S(2)}) copy-start(f32[1,768]{1,0:T(1,128)} %param.21) | copy-start | bytes 9220
  0.7 7.3 %copy-start.36 = (f32[1,768]{1,0:T(1,128)S(1)}, f32[1,768]{1,0:T(1,128)}, u32[]{:S(2)}) copy-start(f32[1,768]{1,0:T(1,128)} %param.22) | copy-start | bytes 9220
  0.7 7.4 %copy-start.32 = (f32[768]{0:T(1024)S(1)}, f32[768]{0:T(1024)}, u32[]{:S(2)}) copy-start(f32[768]{0:T(1024)} %param.20) | copy-start | bytes 9220
  0.7 37.0 %collective-permute-start = (bf16[1000,768]{1,0:T(8,128)(2,1)}, bf16[1000,768]{1,0:T(8,128)(2,1)}, u32[]{:S(2)}, u32[]{:S(2)}) collective-permute-start(bf16[1000,768]{1,0:T(8,128)(2,1)} %bitcast.90), channel_id=1, source_target_pairs={{0,1},{1,0},{2,3},{3,2},{4,5},{5,4},{6,7},{7,6},{8,9},{9,8},{10,11... | collective-permute-start | bytes 4608008 | tf_op jit(solution)/shard_map/ppermute | solution.py:605
  3.8 7.6 %copy-start.4 = (bf16[5,1,200,768]{3,2,1,0:T(8,128)(2,1)S(1)}, bf16[5,1,200,768]{3,2,1,0:T(8,128)(2,1)}, u32[]{:S(2)}) copy-start(bf16[5,1,200,768]{3,2,1,0:T(8,128)(2,1)} %param.13) | copy-start | bytes 4608004
  3.8 7.6 %copy-start.20 = (f32[768]{0:T(1024)S(1)}, f32[768]{0:T(1024)}, u32[]{:S(2)}) copy-start(f32[768]{0:T(1024)} %param.15) | copy-start | bytes 9220
  3.8 7.6 %copy-start.28 = (f32[768]{0:T(1024)S(1)}, f32[768]{0:T(1024)}, u32[]{:S(2)}) copy-start(f32[768]{0:T(1024)} %param.16) | copy-start | bytes 9220
  7.6 7.3 %copy-start.22 = (f32[1000]{0:T(1024)}, f32[1000]{0:T(1024)S(1)}, u32[]{:S(2)}) copy-start(f32[1000]{0:T(1024)S(1)} %div.33) | copy-start | bytes 12004
  8.0 6.9 %copy-start.24 = (f32[1000]{0:T(1024)}, f32[1000]{0:T(1024)S(1)}, u32[]{:S(2)}) copy-start(f32[1000]{0:T(1024)S(1)} %rsqrt.29) | copy-start | bytes 12004
  19.4 26.3 %copy-start.1 = (bf16[1000,2304]{1,0:T(8,128)(2,1)}, bf16[1000,2304]{1,0:T(8,128)(2,1)S(1)}, u32[]{:S(2)}) copy-start(bf16[1000,2304]{1,0:T(8,128)(2,1)S(1)} %convolution_convert_fusion) | copy-start | bytes 13824004
  39.4 6.3 %copy-start.30 = (f32[1000]{0:T(1024)}, f32[1000]{0:T(1024)S(1)}, u32[]{:S(2)}) copy-start(f32[1000]{0:T(1024)S(1)} %broadcast_multiply_fusion.6) | copy-start | bytes 12004
  45.7 23.0 %copy-start.2 = (bf16[1000,1536]{1,0:T(8,128)(2,1)}, bf16[1000,1536]{1,0:T(8,128)(2,1)S(1)}, u32[]{:S(2)}) copy-start(bf16[1000,1536]{1,0:T(8,128)(2,1)S(1)} %convolution_convert_fusion.3) | copy-start | bytes 9216004
  45.7 23.0 %copy-start.5 = (bf16[5,1,200,768]{3,2,1,0:T(8,128)(2,1)S(1)}, bf16[5,1,200,768]{3,2,1,0:T(8,128)(2,1)}, u32[]{:S(2)}) copy-start(bf16[5,1,200,768]{3,2,1,0:T(8,128)(2,1)} %param.13) | copy-start | bytes 4608004
  45.7 23.0 %copy-start.27 = (f32[768]{0:T(1024)S(1)}, f32[768]{0:T(1024)}, u32[]{:S(2)}) copy-start(f32[768]{0:T(1024)} %param.19) | copy-start | bytes 9220
  77.8 35.6 %copy-start.18 = (bf16[5,1,200,768]{3,2,1,0:T(8,128)(2,1)S(1)}, bf16[5,1,200,768]{3,2,1,0:T(8,128)(2,1)}, u32[]{:S(2)}) copy-start(bf16[5,1,200,768]{3,2,1,0:T(8,128)(2,1)} %fusion.37) | copy-start | bytes 4608004
  128.7 9.9 %copy-start.8 = (f32[1000,768]{1,0:T(8,128)S(1)}, f32[1000,768]{1,0:T(8,128)}, u32[]{:S(2)}) copy-start(f32[1000,768]{1,0:T(8,128)} %get-tuple-element.88) | copy-start | bytes 9216004
  128.7 9.9 %copy-start.16 = (bf16[5,1,200,768]{3,2,1,0:T(8,128)(2,1)S(1)}, bf16[5,1,200,768]{3,2,1,0:T(8,128)(2,1)}, u32[]{:S(2)}) copy-start(bf16[5,1,200,768]{3,2,1,0:T(8,128)(2,1)} %param.25) | copy-start | bytes 4608004
  195.8 34.8 %collective-permute-start.1 = (bf16[1000,768]{1,0:T(8,128)(2,1)S(1)}, bf16[1000,768]{1,0:T(8,128)(2,1)S(1)}, u32[]{:S(2)}, u32[]{:S(2)}) collective-permute-start(bf16[1000,768]{1,0:T(8,128)(2,1)S(1)} %get-tuple-element.82), channel_id=1, source_target_pairs={{0,1},{1,0},{2,3},{3,2},{4,5},{5,4},{6,7},{7,6},{8,9},{9,8},{10,11... | collective-permute-start | bytes 4608008 | tf_op jit(solution)/shard_map/ppermute | solution.py:648
  200.2 10.2 %copy-start.9 = (bf16[1,1000,768]{2,1,0:T(8,128)(2,1)S(1)}, bf16[1,1000,768]{2,1,0:T(8,128)(2,1)}, u32[]{:S(2)}) copy-start(bf16[1,1000,768]{2,1,0:T(8,128)(2,1)} %add_convert_fusion.2) | copy-start | bytes 4608004
  210.4 9.5 %slice-start.4 = ((s8[6144000]{0:T(1024)(128)(4,1)}), s8[4194304]{0:T(1024)(128)(4,1)S(1)}, s32[]{:S(2)}) async-start(s8[6144000]{0:T(1024)(128)(4,1)} %bitcast.104), calls=%async_computation.4 | async-start | bytes 8388608
  210.7 6.6 %copy-start.17 = (bf16[5,1,200,768]{3,2,1,0:T(8,128)(2,1)S(1)}, bf16[5,1,200,768]{3,2,1,0:T(8,128)(2,1)}, u32[]{:S(2)}) copy-start(bf16[5,1,200,768]{3,2,1,0:T(8,128)(2,1)} %add_convert_fusion.1) | copy-start | bytes 4608004
  210.7 9.1 %slice-start.5 = ((s8[6144000]{0:T(1024)(128)(4,1)}), s8[1949696]{0:T(1024)(128)(4,1)S(1)}, s32[]{:S(2)}) async-start(s8[6144000]{0:T(1024)(128)(4,1)} %bitcast.104), calls=%async_computation.5 | async-start | bytes 3899392
  219.8 10.8 %copy-start.6 = (bf16[5,1,200,768]{3,2,1,0:T(8,128)(2,1)S(1)}, bf16[5,1,200,768]{3,2,1,0:T(8,128)(2,1)}, u32[]{:S(2)}) copy-start(bf16[5,1,200,768]{3,2,1,0:T(8,128)(2,1)} %param.13) | copy-start | bytes 4608004
  219.8 10.8 %copy-start.23 = (f32[1000]{0:T(1024)S(1)}, f32[1000]{0:T(1024)}, u32[]{:S(2)}) copy-start(f32[1000]{0:T(1024)} %copy-done.22) | copy-start | bytes 12004
  219.8 10.8 %copy-start.25 = (f32[1000]{0:T(1024)S(1)}, f32[1000]{0:T(1024)}, u32[]{:S(2)}) copy-start(f32[1000]{0:T(1024)} %copy-done.24) | copy-start | bytes 12004
  409.1 11.6 %slice-start.2 = ((s8[4718592]{0:T(1024)(128)(4,1)}), s8[4194304]{0:T(1024)(128)(4,1)S(1)}, s32[]{:S(2)}) async-start(s8[4718592]{0:T(1024)(128)(4,1)} %bitcast.94), calls=%async_computation.2 | async-start | bytes 8388608
  413.2 7.4 %slice-start.3 = ((s8[4718592]{0:T(1024)(128)(4,1)}), s8[524288]{0:T(1024)(128)(4,1)S(1)}, s32[]{:S(2)}) async-start(s8[4718592]{0:T(1024)(128)(4,1)} %bitcast.94), calls=%async_computation.3 | async-start | bytes 1048576
  420.7 4.5 %copy-start.13 = (bf16[768,1536]{1,0:T(8,128)(2,1)S(1)}, bf16[768,1536]{1,0:T(8,128)(2,1)}, u32[]{:S(2)}) copy-start(bf16[768,1536]{1,0:T(8,128)(2,1)} %get-tuple-element.28) | copy-start | bytes 7077892
  425.2 5.4 %copy-start.12 = (f32[1000,768]{1,0:T(8,128)S(1)}, f32[1000,768]{1,0:T(8,128)}, u32[]{:S(2)}) copy-start(f32[1000,768]{1,0:T(8,128)} %get-tuple-element.91) | copy-start | bytes 9216004
  425.2 5.8 %copy-start.15 = (bf16[1000,768]{1,0:T(8,128)(2,1)S(1)}, bf16[1000,768]{1,0:T(8,128)(2,1)}, u32[]{:S(2)}) copy-start(bf16[1000,768]{1,0:T(8,128)(2,1)} %copy-done.14) | copy-start | bytes 4608004
  (17 other events, 44.9 us)
